TPU v7x, 32 devices: a whole 2x2x4 slice. The times are simulated.
32 devices in a mesh: gx: 4 (over y, x), gy: 4 (over z), gz: 2 (over core).
Axes of the slice: x: 2, y: 2, z: 4, core: 2. Of those that a mesh axis runs over, the one named last changes fastest.
Arguments:
- densities: float32 [7, 64, 128, 512], P(None, 'gz', 'gy', 'gx'), may hold values from -6 to 6
- residuals: float32 [7, 64, 128, 512], P(None, 'gz', 'gy', 'gx'), may hold values from -320 to 320
Outputs:
- new_density: float32 [64, 128, 512], P('gz', 'gy', 'gx')
- weights: float32 [7], replicated
All inputs are finite; a program needn't handle non-finite values.
Results may differ from a plain program's by a relative error of at most 0.000087.
Values sent between devices are 32-bit elements; how exact they have to be, the bound alone decides.
A program may use at most 64 MiB of HBM per device.

v0:
```python
import functools
import math

import jax
import jax.numpy as jnp
from jax import lax
from jax.experimental import pallas as pl
from jax.experimental.pallas import tpu as pltpu
from jax.sharding import PartitionSpec as P

MESH = pl.DeviceIdType.MESH
SWEEPS = 3
SUB = 8
UNROLL = 4
DEEP = 16
shift_value = 0.15
mix_amount = 0.7
AXES = ("gx", "gy", "gz")


def sweep_weights():
    diag_value = 6.0 + shift_value
    upper = (shift_value + 12.0) / diag_value
    lower = upper / 3.0
    return [
        1.0
        / (
            (upper + lower) / 2.0
            + (upper - lower) / 2.0 * math.cos(math.pi * (2 * k - 1) / (2 * SWEEPS))
        )
        for k in range(1, SWEEPS + 1)
    ]


def kernel(
    counts, dims, chunks,
    res, den, out, wout,
    held, dens, slots, comb, rhs_a, it_a, final, faces, strip, rhs_s, it_s, packs, landed, cfirst, clast,
    in_sem, den_sem, gsend, grecv, zsend, zrecv, ysend, yrecv, xsend, xrecv, csend, crecv,
):
    count, nz, ny, nx = dims
    cx, cy, cz = counts
    total_devices = cx * cy * cz
    zp = nz + SUB
    h = SWEEPS
    ix, iy, iz = (lax.axis_index(a) for a in AXES)
    me = (ix * cy + iy) * cz + iz

    def near(dx, dy, dz):
        return (
            lax.rem(ix + dx + cx, cx),
            lax.rem(iy + dy + cy, cy),
            lax.rem(iz + dz + cz, cz),
        )

    per = nz // chunks
    loads = []
    for c in range(chunks):
        cp = pltpu.make_async_copy(
            res.at[:, pl.ds(c * per, per)], held.at[:, pl.ds(h + c * per, per)], in_sem.at[c]
        )
        cp.start()
        loads.append(cp)
    den_load = pltpu.make_async_copy(den, dens, den_sem)
    den_load.start()

    barrier = pltpu.get_barrier_semaphore()

    offsets = [
        (dx, dy, dz) for dx in range(cx) for dy in range(cy) for dz in range(cz) if dx or dy or dz
    ]
    offsets.sort(key=lambda o: -sum(min(d, c - d) for d, c in zip(o, counts)))
    gx = [lax.rem(ix + d, cx) for d in range(cx)]
    gy = [lax.rem(iy + d, cy) for d in range(cy)]
    gz = [lax.rem(iz + d, cz) for d in range(cz)]
    for dx, dy, dz in offsets:
        pl.semaphore_signal(
            barrier, inc=1, device_id=(gx[dx], gy[dy], gz[dz]), device_id_type=MESH
        )

    @pl.loop(h, ny + h)
    def _(y):
        comb[y, nz:zp, :] = jnp.zeros((SUB, nx), jnp.float32)

    pairs = [(i, j) for i in range(count) for j in range(i, count)]
    tiles = ny // SUB
    accs = tuple(jnp.zeros((SUB, nx), jnp.float32) for _ in pairs)
    for c in range(chunks):
        loads[c].wait()

        def gram_step(z, accs):
            accs = list(accs)
            for t in range(tiles):
                v = [held[i, z, t * SUB:(t + 1) * SUB, :] for i in range(count)]
                for p, (i, j) in enumerate(pairs):
                    accs[p] = accs[p] + v[i] * v[j]
            return tuple(accs)

        accs = lax.fori_loop(h + c * per, h + (c + 1) * per, gram_step, accs)
    lane = lax.broadcasted_iota(jnp.int32, (SUB, nx), 1)
    packed = jnp.zeros((SUB, nx), jnp.float32)
    for p in range(len(pairs)):
        packed = jnp.where(lane == p, jnp.sum(accs[p], axis=1, keepdims=True), packed)
    slots[pl.ds(me, 1)] = jnp.sum(packed, axis=0, keepdims=True).reshape(1, 1, nx)

    pl.semaphore_wait(barrier, total_devices - 1)

    def gram_copy(k, slot):
        dx, dy, dz = offsets[k]
        return pltpu.make_async_remote_copy(
            src_ref=slots.at[me],
            dst_ref=slots.at[slot],
            send_sem=gsend.at[k],
            recv_sem=grecv.at[k],
            device_id=(gx[dx], gy[dy], gz[dz]),
            device_id_type=MESH,
        )

    for k in range(len(offsets)):
        gram_copy(k, me).start()

    zcopies = []
    for k, (start, dest, dz) in enumerate(((h, nz + h, -1), (nz, 0, 1))):
        cp = pltpu.make_async_remote_copy(
            src_ref=held.at[:, pl.ds(start, h)],
            dst_ref=held.at[:, pl.ds(dest, h)],
            send_sem=zsend.at[k],
            recv_sem=zrecv.at[k],
            device_id=near(0, 0, dz),
            device_id_type=MESH,
        )
        cp.start()
        zcopies.append(cp)

    for k, (dx, dy, dz) in enumerate(offsets):
        source = (gx[-dx % cx] * cy + gy[-dy % cy]) * cz + gz[-dz % cz]
        gram_copy(k, source).wait_recv()

    total = jnp.sum(slots[...], axis=0)

    g = {}
    for p, (i, j) in enumerate(pairs):
        g[i, j] = jnp.broadcast_to(total[:, p:p + 1], (SUB, nx))
    b = [jnp.ones((SUB, nx), jnp.float32) for _ in range(count)]
    inv = []
    for k in range(count):
        inv.append(1.0 / g[k, k])
        for i in range(k + 1, count):
            f = g[k, i] * inv[k]
            for j in range(i, count):
                g[i, j] = g[i, j] - f * g[k, j]
            b[i] = b[i] - f * b[k]
    solved = [None] * count
    for k in reversed(range(count)):
        s = b[k]
        for j in range(k + 1, count):
            s = s - g[k, j] * solved[j]
        solved[k] = s * inv[k]
    norm = solved[0]
    for k in range(1, count):
        norm = norm + solved[k]
    weights = [s / norm for s in solved]
    row = jnp.zeros((SUB, nx), jnp.float32)
    for k in range(count):
        row = jnp.where(lane == k, weights[k], row)
    wout[...] = row[0:1, :count]

    flat = comb.reshape((ny + 2 * h) * zp, nx)

    def combine(z, row):
        for t in range(tiles):
            s = weights[0] * held[0, z, t * SUB:(t + 1) * SUB, :]
            for i in range(1, count):
                s = s + weights[i] * held[i, z, t * SUB:(t + 1) * SUB, :]
            flat[pl.ds((h + t * SUB) * zp + row, SUB, stride=zp), :] = s

    @pl.loop(0, nz)
    def _(z):
        combine(z + h, z)

    for cp in zcopies:
        cp.wait()
    for j in range(h):
        combine(j, zp - h + j)
        combine(nz + h + j, nz + j)

    ztiles = zp // SUB
    width = 6 * h
    group = lane // width
    inner = lane - width * group
    at_left = inner < 3 * h

    def own_strip(e):
        total = jnp.zeros((SUB, nx), jnp.float32)
        for zt in range(ztiles):
            v = comb[e, zt * SUB:(zt + 1) * SUB, :]
            near_left = pltpu.roll(v, (width * zt + h) % nx, 1)
            near_right = pltpu.roll(v, (width * zt + 5 * h) % nx, 1)
            total = jnp.where(group == zt, jnp.where(at_left, near_left, near_right), total)
        strip[e] = total

    def planes(start, stop, unroll):
        steps = (stop - start) // unroll

        def wrap(body):
            @pl.loop(0, steps)
            def _(it):
                for r in range(unroll):
                    body(start + it * unroll + r)

            for e in range(start + steps * unroll, stop):
                body(e)
            return body

        return wrap

    planes(h, ny + h, 8)(own_strip)

    each = width // h
    place = inner // h
    for m in range(packs.shape[1]):
        head = jnp.zeros((SUB, nx), jnp.float32)
        tail = jnp.zeros((SUB, nx), jnp.float32)
        for q in range(min(each, ny - m * each)):
            v = strip[h + m * each + q]
            head = jnp.where(place == q, pltpu.roll(v, (h * q - h) % nx, 1), head)
            tail = jnp.where(place == q, pltpu.roll(v, (h * q - 4 * h) % nx, 1), tail)
        packs[0, m] = head
        packs[1, m] = tail

    low = (ny - h) // each
    xcopies = []

    def send_x(source, target, send_sem, recv_sem, dx, dy):
        cp = pltpu.make_async_remote_copy(
            src_ref=source,
            dst_ref=target,
            send_sem=send_sem,
            recv_sem=recv_sem,
            device_id=near(dx, dy, 0),
            device_id_type=MESH,
        )
        cp.start()
        xcopies.append(cp)

    for k, dx in enumerate((-1, 1)):
        send_x(
            packs.at[k, pl.ds(low, clast.shape[1])], clast.at[k],
            csend.at[k, 0], crecv.at[k, 0], dx, 1,
        )
        send_x(
            packs.at[k, pl.ds(0, cfirst.shape[1])], cfirst.at[k],
            csend.at[k, 1], crecv.at[k, 1], dx, -1,
        )
    for k, dx in enumerate((-1, 1)):
        send_x(packs.at[k], landed.at[k], xsend.at[k], xrecv.at[k], dx, 0)

    ycopies = []
    for k, (start, dest, dy) in enumerate(((h, ny + h, -1), (ny, 0, 1))):
        cp = pltpu.make_async_remote_copy(
            src_ref=comb.at[pl.ds(start, h)],
            dst_ref=comb.at[pl.ds(dest, h)],
            send_sem=ysend.at[k],
            recv_sem=yrecv.at[k],
            device_id=near(0, dy, 0),
            device_id_type=MESH,
        )
        cp.start()
        ycopies.append(cp)

    den_load.wait()

    @pl.loop(0, nz)
    def _(z):
        for t in range(tiles):
            s = weights[0] * dens[0, z, t * SUB:(t + 1) * SUB, :]
            for i in range(1, count):
                s = s + weights[i] * dens[i, z, t * SUB:(t + 1) * SUB, :]
            out[z, t * SUB:(t + 1) * SUB, :] = s

    def around(f, e):
        v = f[e]
        total = pltpu.roll(v, 1, 1) + pltpu.roll(v, nx - 1, 1)
        total = total + (pltpu.roll(v, 1, 0) + pltpu.roll(v, zp - 1, 0))
        return v, total + (f[e - 1] + f[e + 1])

    diag_value = 6.0 + shift_value
    w1, w2, w3 = sweep_weights()
    alpha = ((1.0 - w2) * w1 + w2) / diag_value
    beta = w1 * w2 / (diag_value * diag_value)

    def first_pass(e):
        v, total = around(comb, e)
        rhs_a[e] = 6.0 * v - total

    planes(h + 1, ny + h - 1, UNROLL)(first_pass)

    def second_pass(e):
        v, total = around(rhs_a, e)
        it_a[e] = alpha * v + beta * total

    planes(h + 2, ny + h - 2, UNROLL)(second_pass)

    edge = (lane < h) | (lane >= nx - h)

    def last_step(v, total, r):
        return (mix_amount * (1.0 - w3)) * v + (mix_amount * w3 / diag_value) * (r + total)

    def third_pass(e):
        v, total = around(it_a, e)
        u = last_step(v, total, rhs_a[e])
        for zt in range(nz // SUB):
            rows = slice(zt * SUB, (zt + 1) * SUB)
            final[e, rows, :] = u[rows, :]

    planes(h + 3, ny + h - 3, UNROLL)(third_pass)

    for cp in ycopies:
        cp.wait()

    for e in (*range(h), *range(ny + h, ny + 2 * h)):
        own_strip(e)
    for e in (*range(1, h + 1), *range(ny + h - 1, ny + 2 * h - 1)):
        first_pass(e)
    for e in (*range(2, h + 2), *range(ny + h - 2, ny + 2 * h - 2)):
        second_pass(e)
    for e in (*range(h, h + 3), *range(ny + h - 3, ny + h)):
        third_pass(e)

    for cp in xcopies:
        cp.wait()

    for e in range(ny + 2 * h):
        if e < h:
            ref, y, m0 = clast, ny - h + e, low
        elif e < ny + h:
            ref, y, m0 = landed, e - h, 0
        else:
            ref, y, m0 = cfirst, e - h - ny, 0
        m, q = y // each - m0, y % each
        head = pltpu.roll(ref[0, m], (5 * h - h * q) % nx, 1)
        tail = pltpu.roll(ref[1, m], (-h * q) % nx, 1)
        strip[e] = jnp.where(inner < h, tail, jnp.where(inner >= 5 * h, head, strip[e]))

    sub = lax.broadcasted_iota(jnp.int32, (SUB, nx), 0)
    wrap_by = (ztiles - 1) * width

    def around_strip(f, e):
        v = f[e]
        total = pltpu.roll(v, 1, 1) + pltpu.roll(v, nx - 1, 1)
        below = pltpu.roll(v, 1, 0)
        carried = jnp.where(
            group == 0, pltpu.roll(below, nx - wrap_by, 1), pltpu.roll(below, width, 1)
        )
        total = total + jnp.where(sub == 0, carried, below)
        above = pltpu.roll(v, SUB - 1, 0)
        carried = jnp.where(
            group == ztiles - 1, pltpu.roll(above, wrap_by, 1), pltpu.roll(above, nx - width, 1)
        )
        total = total + jnp.where(sub == SUB - 1, carried, above)
        return v, total + (f[e - 1] + f[e + 1])

    @planes(1, ny + 2 * h - 1, DEEP)
    def _(e):
        v, total = around_strip(strip, e)
        rhs_s[e] = 6.0 * v - total

    @planes(2, ny + 2 * h - 2, DEEP)
    def _(e):
        v, total = around_strip(rhs_s, e)
        it_s[e] = alpha * v + beta * total

    def last_strips(e):
        v, total = around_strip(it_s, e)
        u = last_step(v, total, rhs_s[e])
        u = jnp.where(inner < h, pltpu.roll(u, nx - 4 * h, 1), u)
        for zt in range(nz // SUB):
            faces[e, zt * SUB:(zt + 1) * SUB, :] = pltpu.roll(u, (-(width * zt + h)) % nx, 1)

    planes(h, ny + h, DEEP)(last_strips)

    flat_final = final.reshape((ny + 2 * h) * zp, nx)
    flat_faces = faces.reshape((ny + 2 * h) * zp, nx)

    @pl.loop(0, nz // 4)
    def _(block):
        for r in range(4):
            z = block * 4 + r
            for t in range(tiles):
                rows = pl.ds((h + t * SUB) * zp + z, SUB, stride=zp)
                u = jnp.where(edge, flat_faces[rows, :], flat_final[rows, :])
                out[z, t * SUB:(t + 1) * SUB, :] = out[z, t * SUB:(t + 1) * SUB, :] + u

    for k in range(len(offsets)):
        gram_copy(k, me).wait_send()


def hand_over(mixed, weights, out, wout, sem):
    pieces = sem.shape[0]
    per = mixed.shape[0] // pieces
    copies = []
    for c in range(pieces):
        part = pl.ds(c * per, per)
        cp = pltpu.make_async_copy(mixed.at[part], out.at[part], sem.at[c])
        cp.start()
        copies.append(cp)
    wout[...] = weights[...]
    for cp in copies:
        cp.wait()


def on_device(counts, densities, residuals):
    dims = residuals.shape
    count, nz, ny, nx = dims
    h = SWEEPS
    zp = nz + SUB
    n = counts[0] * counts[1] * counts[2]
    chunks = 4
    field = pltpu.VMEM((ny + 2 * h, zp, nx), jnp.float32)
    strips = pltpu.VMEM((ny + 2 * h, SUB, nx), jnp.float32)
    each = 6
    messages = pl.cdiv(ny, each)
    dma = pltpu.SemaphoreType.DMA

    def faces(blocks):
        return pltpu.VMEM((2, blocks, SUB, nx), jnp.float32)

    any_spec = pl.BlockSpec(memory_space=pl.ANY)
    vmem = pl.BlockSpec(memory_space=pltpu.VMEM)
    new_density, weights = pl.pallas_call(
        functools.partial(kernel, counts, dims, chunks),
        out_shape=(
            pltpu.VMEM((nz, ny, nx), jnp.float32),
            pltpu.VMEM((1, count), jnp.float32),
        ),
        in_specs=[any_spec, any_spec],
        out_specs=(vmem, vmem),
        scratch_shapes=[
            pltpu.VMEM((count, nz + 2 * h, ny, nx), jnp.float32),
            pltpu.VMEM(dims, jnp.float32),
            pltpu.VMEM((n, 1, nx), jnp.float32),
            field, field, field, field, field, strips, strips, strips,
            faces(messages),
            faces(messages),
            faces(pl.cdiv(h, each)),
            faces(messages - (ny - h) // each),
            dma((chunks,)), dma(()), dma((n,)), dma((n,)),
            dma((2,)), dma((2,)), dma((2,)), dma((2,)), dma((2,)), dma((2,)), dma((2, 2)), dma((2, 2)),
        ],
        compiler_params=pltpu.CompilerParams(
            collective_id=0, has_side_effects=True, vmem_limit_bytes=61 * 1024 * 1024
        ),
    )(residuals, densities)
    new_density, weights = pl.pallas_call(
        hand_over,
        out_shape=(
            jax.ShapeDtypeStruct((nz, ny, nx), jnp.float32),
            jax.ShapeDtypeStruct((1, count), jnp.float32),
        ),
        in_specs=[vmem, vmem],
        out_specs=(any_spec, vmem),
        scratch_shapes=[dma((4,))],
        compiler_params=pltpu.CompilerParams(vmem_limit_bytes=4 * 1024 * 1024),
    )(new_density, weights)
    return new_density, weights.reshape(count)


def solution(mesh):
    counts = tuple(mesh.shape[a] for a in AXES)
    placed = (P(None, "gz", "gy", "gx"), P(None, "gz", "gy", "gx"))
    return jax.shard_map(
        functools.partial(on_device, counts),
        mesh=mesh,
        in_specs=placed,
        out_specs=(P("gz", "gy", "gx"), P()),
        check_vma=False,
    )
```

profile of v0, /device:TPU:0, one launch (start us, length us, event | category | flops | bytes accessed | tf_op | source)
XLA Modules:
  0.0 23.1 jit_solution(10036473987067922)
XLA Ops:
  0.6 21.1 %shard_map.41 = (f32[32,32,128]{2,1,0:T(8,128)S(1)}, f32[1,7]{1,0:T(1,128)S(1)}) custom-call(f32[7,32,32,128]{3,2,1,0:T(8,128)} %res.1, f32[7,32,32,128]{3,2,1,0:T(8,128)} %den.1), custom_call_target="tpu_custom_call" | custom-call | tf_op jit(solution)/shard_map/pallas_call | solution.py:430
  21.8 1.3 %shard_map.42 = (f32[32,32,128]{2,1,0:T(8,128)}, f32[1,7]{1,0:T(1,128)}) custom-call(f32[32,32,128]{2,1,0:T(8,128)S(1)} %get-tuple-element.6.mixed, f32[1,7]{1,0:T(1,128)S(1)} %get-tuple-element.7.weights), custom_call_target="tpu_custom_call" | custom-call | tf_op jit(solution)/shard_map/pallas_call | solution.py:454
where the time goes:
time: 23.3 us; the launch traced here: 23.1 us
  Pallas kernels  22.5 us (97%)
  between operations  0.64 us (3%)
    pallas_call x1, Pallas kernels, on_device(): pl.pallas_call(functools.partial(kernel, counts, dims, chunks), out_shape...  21.1 us
    pallas_call x1, Pallas kernels, on_device(): pl.pallas_call(hand_over, out_shape=(jax.ShapeDtypeStruct((nz, ny, nx), j...  1.33 us

commit v1 on v0

v1 whole, which is shorter than its diff:
```python
import functools
import math

import jax
import jax.numpy as jnp
from jax import lax
from jax.experimental import pallas as pl
from jax.experimental.pallas import tpu as pltpu
from jax.sharding import PartitionSpec as P

MESH = pl.DeviceIdType.MESH
SWEEPS = 3
SUB = 8
UNROLL = 4
shift_value = 0.15
mix_amount = 0.7
AXES = ("gx", "gy", "gz")


def sweep_weights():
    diag_value = 6.0 + shift_value
    upper = (shift_value + 12.0) / diag_value
    lower = upper / 3.0
    return [
        1.0
        / (
            (upper + lower) / 2.0
            + (upper - lower) / 2.0 * math.cos(math.pi * (2 * k - 1) / (2 * SWEEPS))
        )
        for k in range(1, SWEEPS + 1)
    ]


def sweep_factors():
    diag_value = 6.0 + shift_value
    w1, w2, w3 = sweep_weights()
    alpha = ((1.0 - w2) * w1 + w2) / diag_value
    beta = w1 * w2 / (diag_value * diag_value)
    return alpha, beta, mix_amount * (1.0 - w3), mix_amount * w3 / diag_value


def neighbour_polynomial():
    alpha, beta, keep, step = sweep_factors()
    q0 = keep * alpha + step
    q1 = keep * beta + step * alpha
    q2 = step * beta
    return 6.0 * q0, 6.0 * q1 - q0, 6.0 * q2 - q1, -q2


def kernel(
    counts, dims, chunks,
    res, den, base, xc, yc, wout,
    held, dens, slots, comb, rhs, it, raw, pack, land, ybuf, yland,
    in_sem, den_sem, gsend, grecv, zsend, zrecv, ysend, yrecv, xsend, xrecv, csend, crecv,
):
    count, nz, ny, nx = dims
    cx, cy, cz = counts
    total_devices = cx * cy * cz
    h = SWEEPS
    ze = nz + 2 * h
    zp = yland.shape[1] // h
    tiles = ny // SUB
    ix, iy, iz = (lax.axis_index(a) for a in AXES)
    me = (ix * cy + iy) * cz + iz

    def near(dx, dy, dz):
        return (
            lax.rem(ix + dx + cx, cx),
            lax.rem(iy + dy + cy, cy),
            lax.rem(iz + dz + cz, cz),
        )

    per = nz // chunks
    loads = []
    for c in range(chunks):
        cp = pltpu.make_async_copy(
            res.at[:, pl.ds(c * per, per)], held.at[:, pl.ds(h + c * per, per)], in_sem.at[c]
        )
        cp.start()
        loads.append(cp)

    barrier = pltpu.get_barrier_semaphore()

    offsets = [
        (dx, dy, dz) for dx in range(cx) for dy in range(cy) for dz in range(cz) if dx or dy or dz
    ]
    offsets.sort(key=lambda o: -sum(min(d, c - d) for d, c in zip(o, counts)))
    gx = [lax.rem(ix + d, cx) for d in range(cx)]
    gy = [lax.rem(iy + d, cy) for d in range(cy)]
    gz = [lax.rem(iz + d, cz) for d in range(cz)]
    for dx, dy, dz in offsets:
        pl.semaphore_signal(
            barrier, inc=1, device_id=(gx[dx], gy[dy], gz[dz]), device_id_type=MESH
        )

    pairs = [(i, j) for i in range(count) for j in range(i, count)]
    accs = tuple(jnp.zeros((SUB, nx), jnp.float32) for _ in pairs)
    den_load = pltpu.make_async_copy(den, dens, den_sem)
    for c in range(chunks):
        loads[c].wait()
        if c == chunks - 1:
            den_load.start()

        def gram_step(z, accs):
            accs = list(accs)
            for t in range(tiles):
                v = [held[i, z, t * SUB:(t + 1) * SUB, :] for i in range(count)]
                for p, (i, j) in enumerate(pairs):
                    accs[p] = accs[p] + v[i] * v[j]
            return tuple(accs)

        accs = lax.fori_loop(h + c * per, h + (c + 1) * per, gram_step, accs)
    lane = lax.broadcasted_iota(jnp.int32, (SUB, nx), 1)
    packed = jnp.zeros((SUB, nx), jnp.float32)
    for p in range(len(pairs)):
        packed = jnp.where(lane == p, jnp.sum(accs[p], axis=1, keepdims=True), packed)
    slots[pl.ds(me, 1)] = jnp.sum(packed, axis=0, keepdims=True).reshape(1, 1, nx)

    pl.semaphore_wait(barrier, total_devices - 1)

    def gram_copy(k, slot):
        dx, dy, dz = offsets[k]
        return pltpu.make_async_remote_copy(
            src_ref=slots.at[me],
            dst_ref=slots.at[slot],
            send_sem=gsend.at[k],
            recv_sem=grecv.at[k],
            device_id=(gx[dx], gy[dy], gz[dz]),
            device_id_type=MESH,
        )

    for k in range(len(offsets)):
        gram_copy(k, me).start()

    zcopies = []
    for k, (start, dest, dz) in enumerate(((h, nz + h, -1), (nz, 0, 1))):
        cp = pltpu.make_async_remote_copy(
            src_ref=held.at[:, pl.ds(start, h)],
            dst_ref=held.at[:, pl.ds(dest, h)],
            send_sem=zsend.at[k],
            recv_sem=zrecv.at[k],
            device_id=near(0, 0, dz),
            device_id_type=MESH,
        )
        cp.start()
        zcopies.append(cp)

    third = lane // h

    def gather_faces(rows, fresh):
        @pl.loop(0, count)
        def _(i):
            for t in range(tiles):
                span = slice(t * SUB, (t + 1) * SUB)
                if fresh:
                    head = jnp.zeros((SUB, nx), jnp.float32)
                    tail = head
                else:
                    head, tail = raw[i, 0, span, :], raw[i, 1, span, :]
                for z in rows:
                    v = pltpu.roll(held[i, z, span, :], h * z + h, 1)
                    head = jnp.where(third == z + 1, v, head)
                    tail = jnp.where(third == z, v, tail)
                raw[i, 0, span, :] = head
                raw[i, 1, span, :] = tail

    gather_faces(range(h, nz + h), True)

    for p in range(h, SUB):
        yc[p * zp:(p + 1) * zp, :] = jnp.zeros((zp, nx), jnp.float32)
        mirror = 2 * SUB - 1 - p
        yc[mirror * zp:(mirror + 1) * zp, :] = jnp.zeros((zp, nx), jnp.float32)

    for cp in zcopies:
        cp.wait()
    gather_faces((*range(h), *range(nz + h, ze)), False)

    for k, (dx, dy, dz) in enumerate(offsets):
        source = (gx[-dx % cx] * cy + gy[-dy % cy]) * cz + gz[-dz % cz]
        gram_copy(k, source).wait_recv()

    total = jnp.sum(slots[...], axis=0)

    g = {}
    for p, (i, j) in enumerate(pairs):
        g[i, j] = jnp.broadcast_to(total[:, p:p + 1], (SUB, nx))
    b = [jnp.ones((SUB, nx), jnp.float32) for _ in range(count)]
    inv = []
    for k in range(count):
        inv.append(1.0 / g[k, k])
        for i in range(k + 1, count):
            f = g[k, i] * inv[k]
            for j in range(i, count):
                g[i, j] = g[i, j] - f * g[k, j]
            b[i] = b[i] - f * b[k]
    solved = [None] * count
    for k in reversed(range(count)):
        s = b[k]
        for j in range(k + 1, count):
            s = s - g[k, j] * solved[j]
        solved[k] = s * inv[k]
    norm = solved[0]
    for k in range(1, count):
        norm = norm + solved[k]
    weights = [s / norm for s in solved]

    for k in range(2):
        for t in range(tiles):
            span = slice(t * SUB, (t + 1) * SUB)
            s = weights[0] * raw[0, k, span, :]
            for i in range(1, count):
                s = s + weights[i] * raw[i, k, span, :]
            pack[k, span, :] = s

    copies = []

    def send(source, target, send_sem, recv_sem, dx, dy):
        cp = pltpu.make_async_remote_copy(
            src_ref=source,
            dst_ref=target,
            send_sem=send_sem,
            recv_sem=recv_sem,
            device_id=near(dx, dy, 0),
            device_id_type=MESH,
        )
        cp.start()
        copies.append(cp)

    for k, dx in enumerate((-1, 1)):
        side = land.at[1 - k]
        send(
            pack.at[k, pl.ds(ny - SUB, SUB)], side.at[pl.ds(0, SUB)],
            csend.at[k, 0], crecv.at[k, 0], dx, 1,
        )
        send(
            pack.at[k, pl.ds(0, SUB)], side.at[pl.ds(ny + SUB, SUB)],
            csend.at[k, 1], crecv.at[k, 1], dx, -1,
        )
    for k, dx in enumerate((-1, 1)):
        send(pack.at[k], land.at[1 - k, pl.ds(SUB, ny)], xsend.at[k], xrecv.at[k], dx, 0)

    def combine(z, t):
        span = slice(t * SUB, (t + 1) * SUB)
        s = weights[0] * held[0, z, span, :]
        for i in range(1, count):
            s = s + weights[i] * held[i, z, span, :]
        comb[z, span, :] = s
        return s

    @pl.loop(0, ze // 2)
    def _(half):
        for r in range(2):
            z = half * 2 + r
            for k, t in enumerate((0, tiles - 1)):
                ybuf[pl.ds(k * SUB * zp + z, SUB, stride=zp), :] = combine(z, t)

    for k, (start, dy) in enumerate(((0, -1), ((2 * SUB - h) * zp, 1))):
        send(
            ybuf.at[pl.ds(start, h * zp)], yland.at[1 - k],
            ysend.at[k], yrecv.at[k], 0, dy,
        )

    @pl.loop(0, ze // 2)
    def _(half):
        for r in range(2):
            for t in range(1, tiles - 1):
                combine(half * 2 + r, t)

    row = jnp.zeros((SUB, nx), jnp.float32)
    for k in range(count):
        row = jnp.where(lane == k, weights[k], row)
    wout[...] = row[0:1, :count]

    def around(f, z):
        v = f[z]
        total = pltpu.roll(v, 1, 1) + pltpu.roll(v, nx - 1, 1)
        total = total + (pltpu.roll(v, 1, 0) + pltpu.roll(v, ny - 1, 0))
        return v, total + (f[z - 1] + f[z + 1])

    def planes(start, stop, unroll):
        steps = (stop - start) // unroll

        def wrap(body):
            @pl.loop(0, steps)
            def _(block):
                for r in range(unroll):
                    body(start + block * unroll + r)

            for z in range(start + steps * unroll, stop):
                body(z)
            return body

        return wrap

    alpha, beta, keep, step = sweep_factors()

    @planes(1, ze - 1, UNROLL)
    def _(z):
        v, total = around(comb, z)
        rhs[z] = 6.0 * v - total

    @planes(2, ze - 2, UNROLL)
    def _(z):
        v, total = around(rhs, z)
        it[z] = alpha * v + beta * total

    den_load.wait()

    @planes(h, nz + h, UNROLL)
    def _(z):
        v, total = around(it, z)
        u = keep * v + step * (rhs[z] + total)
        for t in range(tiles):
            span = slice(t * SUB, (t + 1) * SUB)
            s = weights[0] * dens[0, z - h, span, :]
            for i in range(1, count):
                s = s + weights[i] * dens[i, z - h, span, :]
            base[z - h, span, :] = s + u[span, :]

    for cp in copies:
        cp.wait()

    _, c1, c2, c3 = neighbour_polynomial()

    def by_distance(first, second, square):
        near_by = (c1 + 3.0 * c3) * first + (2.0 * c2) * second + (3.0 * c3) * square
        return near_by, c2 * first + (3.0 * c3) * second

    wide = ny + 2 * SUB
    inside = slice(SUB, SUB + ny)
    column = lax.broadcasted_iota(jnp.int32, (ny, nx), 1)
    place = column % h

    def plane_sum(d):
        total = pltpu.roll(d, h, 1) + pltpu.roll(d, nx - h, 1)
        return total + (pltpu.roll(d, 1, 0) + pltpu.roll(d, wide - 1, 0))

    sides = []
    for s in range(2):
        own = pack[1 - s]
        d = land[s] - jnp.concatenate([own[ny - SUB:], own, own[:SUB]], axis=0)
        m = plane_sum(d)
        mm = plane_sum(m)
        a1, a2 = by_distance(d[inside], m[inside], mm[inside])
        a3 = c3 * d[inside]
        if s == 0:
            a1, a2, a3 = (pltpu.roll(a, k + 1, 1) for k, a in enumerate((a1, a2, a3)))
            depth = place
        else:
            a1, a2, a3 = (pltpu.roll(a, nx - k - 1, 1) for k, a in enumerate((a1, a2, a3)))
            depth = (h - 1) - place
        sides.append(
            jnp.where(depth == 0, a1, 0.0) + jnp.where(depth <= 1, a2, 0.0) + a3
        )
    even = (column // h) % 2 == 0
    xc[0] = jnp.where(even, sides[1], sides[0])
    xc[1] = jnp.where(even, sides[0], sides[1])

    along = lax.broadcasted_iota(jnp.int32, (zp, nx), 1)
    at_first, at_last = along == 0, along == nx - 1

    def face_sum(d):
        total = jnp.where(at_first, 0.0, pltpu.roll(d, 1, 1))
        total = total + jnp.where(at_last, 0.0, pltpu.roll(d, nx - 1, 1))
        return total + (pltpu.roll(d, 1, 0) + pltpu.roll(d, zp - 1, 0))

    for s in range(2):
        ds = []
        for k in range(h):
            p = h - 1 - k if s == 0 else k
            q = 2 * SUB - 1 - k if s == 0 else k
            ds.append(yland[s, p * zp:(p + 1) * zp, :] - ybuf[q * zp:(q + 1) * zp, :])
        m = face_sum(ds[0])
        mm = face_sum(m) + jnp.where(at_first | at_last, ds[0], 0.0)
        near_1, near_2 = by_distance(ds[0], m, mm)
        rows = [
            near_1 + (c2 * ds[1] + (3.0 * c3) * face_sum(ds[1])) + c3 * ds[2],
            near_2 + c3 * ds[1],
            c3 * ds[0],
        ]
        for j, r in enumerate(rows):
            p = j if s == 0 else 2 * SUB - 1 - j
            yc[p * zp:(p + 1) * zp, :] = r

    for k in range(len(offsets)):
        gram_copy(k, me).wait_send()


def finish(base, xc, yc, weights, out, wout, stage, sem, wsem):
    nz, ny, nx = base.shape
    h = SWEEPS
    zp = yc.shape[0] // (2 * SUB)
    tiles = ny // SUB
    pieces = sem.shape[0]
    per = nz // pieces
    wcopy = pltpu.make_async_copy(weights, wout, wsem)
    wcopy.start()
    lane = lax.broadcasted_iota(jnp.int32, (SUB, nx), 1)
    edge = (lane < h) | (lane >= nx - h)
    copies = []
    for c in range(pieces):
        for z in range(c * per, (c + 1) * per):
            e = z + h
            for t in range(tiles):
                span = slice(t * SUB, (t + 1) * SUB)
                v = pltpu.roll(xc[e % 2, span, :], (-(h * e + h)) % nx, 1)
                v = base[z, span, :] + jnp.where(edge, v, 0.0)
                if t == 0:
                    v = v + yc[pl.ds(e, SUB, stride=zp), :]
                if t == tiles - 1:
                    v = v + yc[pl.ds(SUB * zp + e, SUB, stride=zp), :]
                stage[z, span, :] = v
        part = pl.ds(c * per, per)
        cp = pltpu.make_async_copy(stage.at[part], out.at[part], sem.at[c])
        cp.start()
        copies.append(cp)
    for cp in copies:
        cp.wait()
    wcopy.wait()


def on_device(counts, densities, residuals):
    dims = residuals.shape
    count, nz, ny, nx = dims
    h = SWEEPS
    ze = nz + 2 * h
    zp = pl.cdiv(ze, SUB) * SUB
    n = counts[0] * counts[1] * counts[2]
    chunks = 8
    tiles = ny // SUB
    assert tiles >= 2 and h * (ze + 1) <= nx
    dma = pltpu.SemaphoreType.DMA
    f32 = jnp.float32
    field = pltpu.VMEM((ze, ny, nx), f32)

    any_spec = pl.BlockSpec(memory_space=pl.ANY)
    vmem = pl.BlockSpec(memory_space=pltpu.VMEM)
    parts = pl.pallas_call(
        functools.partial(kernel, counts, dims, chunks),
        out_shape=(
            pltpu.VMEM((nz, ny, nx), f32),
            pltpu.VMEM((2, ny, nx), f32),
            pltpu.VMEM((2 * SUB * zp, nx), f32),
            pltpu.VMEM((1, count), f32),
        ),
        in_specs=[any_spec, any_spec],
        out_specs=(vmem, vmem, vmem, vmem),
        scratch_shapes=[
            pltpu.VMEM((count, ze, ny, nx), f32),
            pltpu.VMEM(dims, f32),
            pltpu.VMEM((n, 1, nx), f32),
            field, field, field,
            pltpu.VMEM((count, 2, ny, nx), f32),
            pltpu.VMEM((2, ny, nx), f32),
            pltpu.VMEM((2, ny + 2 * SUB, nx), f32),
            pltpu.VMEM((2 * SUB * zp, nx), f32),
            pltpu.VMEM((2, h * zp, nx), f32),
            dma((chunks,)), dma(()), dma((n,)), dma((n,)),
            dma((2,)), dma((2,)), dma((2,)), dma((2,)), dma((2,)), dma((2,)), dma((2, 2)), dma((2, 2)),
        ],
        compiler_params=pltpu.CompilerParams(
            collective_id=0, has_side_effects=True, vmem_limit_bytes=56 * 1024 * 1024
        ),
    )(residuals, densities)
    new_density, weights = pl.pallas_call(
        finish,
        out_shape=(
            jax.ShapeDtypeStruct((nz, ny, nx), f32),
            jax.ShapeDtypeStruct((1, count), f32),
        ),
        in_specs=[vmem, vmem, vmem, vmem],
        out_specs=(any_spec, any_spec),
        scratch_shapes=[pltpu.VMEM((nz, ny, nx), f32), dma((8,)), dma(())],
        compiler_params=pltpu.CompilerParams(vmem_limit_bytes=4 * 1024 * 1024),
    )(*parts)
    return new_density, weights.reshape(count)


def solution(mesh):
    counts = tuple(mesh.shape[a] for a in AXES)
    placed = (P(None, "gz", "gy", "gx"), P(None, "gz", "gy", "gx"))
    return jax.shard_map(
        functools.partial(on_device, counts),
        mesh=mesh,
        in_specs=placed,
        out_specs=(P("gz", "gy", "gx"), P()),
        check_vma=False,
    )
```

time: 23.3 us -> 19.6 us (0.84)
  Pallas kernels: 22.5 us -> 18.8 us
    pallas_call x1, Pallas kernels: 21.1 us -> 17.9 us  [on_device(): pl.pallas_call(functools.partial(kernel, counts, dims, chunks), out_shape...]
    pallas_call x1, Pallas kernels: 1.33 us -> 0.95 us  [on_device(): pl.pallas_call(finish, out_shape=(jax.ShapeDtypeStruct((nz, ny, nx), f32)...]
where the time goes in v1:
time: 19.6 us; the launch traced here: 19.5 us
  Pallas kernels  18.8 us (96%)
  between operations  0.64 us (3%)
    pallas_call x1, Pallas kernels, on_device(): pl.pallas_call(functools.partial(kernel, counts, dims, chunks), out_shape...  17.9 us
    pallas_call x1, Pallas kernels, on_device(): pl.pallas_call(finish, out_shape=(jax.ShapeDtypeStruct((nz, ny, nx), f32)...  0.95 us

profile of v1, /device:TPU:0, one launch (start us, length us, event | category | flops | bytes accessed | tf_op | source)
XLA Modules:
  0.0 19.5 jit_solution(888504522111135150)
XLA Ops:
  0.6 17.9 %shard_map.41 = (f32[32,32,128]{2,1,0:T(8,128)S(1)}, f32[2,32,128]{2,1,0:T(8,128)S(1)}, f32[640,128]{1,0:T(8,128)S(1)}, f32[1,7]{1,0:T(1,128)S(1)}) custom-call(f32[7,32,32,128]{3,2,1,0:T(8,128)} %res.1, f32[7,32,32,128]{3,2,1,0:T(8,128)} %den.1), custom_call_target="tpu_custom_call" | custom-call | tf_op jit(solution)/shard_map/pallas_call | solution.py:438
  18.5 0.9 %shard_map.42 = (f32[32,32,128]{2,1,0:T(8,128)}, f32[1,7]{1,0:T(1,128)}) custom-call(f32[32,32,128]{2,1,0:T(8,128)S(1)} %get-tuple-element.8.base, f32[2,32,128]{2,1,0:T(8,128)S(1)} %get-tuple-element.9.xc, f32[640,128]{1,0:T(8,128)S(1)} %get-tuple-element.10.yc, f32[1,7]{1,0:T(1,128)S(1)} %get-tuple-element.11.weights), custom_call_target="tpu_custom_call" | custom-call | tf_op jit(solution)/shard_map/pallas_call | solution.py:465

commit v2 on v1

--- a/solution.py
+++ b/solution.py
@@ -49,8 +49,8 @@
 
 def kernel(
     counts, dims, chunks,
-    res, den, base, xc, yc, wout,
-    held, dens, slots, comb, rhs, it, raw, pack, land, ybuf, yland,
+    res, den, base, yc, wout,
+    held, dens, slots, comb, rhs, it, raw, pack, land, cland, yraw, ybuf, yland, xc,
     in_sem, den_sem, gsend, grecv, zsend, zrecv, ysend, yrecv, xsend, xrecv, csend, crecv,
 ):
     count, nz, ny, nx = dims
@@ -70,15 +70,6 @@
             lax.rem(iz + dz + cz, cz),
         )
 
-    per = nz // chunks
-    loads = []
-    for c in range(chunks):
-        cp = pltpu.make_async_copy(
-            res.at[:, pl.ds(c * per, per)], held.at[:, pl.ds(h + c * per, per)], in_sem.at[c]
-        )
-        cp.start()
-        loads.append(cp)
-
     barrier = pltpu.get_barrier_semaphore()
 
     offsets = [
@@ -93,6 +84,15 @@
             barrier, inc=1, device_id=(gx[dx], gy[dy], gz[dz]), device_id_type=MESH
         )
 
+    per = nz // chunks
+    loads = []
+    for c in range(chunks):
+        cp = pltpu.make_async_copy(
+            res.at[:, pl.ds(c * per, per)], held.at[:, pl.ds(h + c * per, per)], in_sem.at[c]
+        )
+        cp.start()
+        loads.append(cp)
+
     pairs = [(i, j) for i in range(count) for j in range(i, count)]
     accs = tuple(jnp.zeros((SUB, nx), jnp.float32) for _ in pairs)
     den_load = pltpu.make_async_copy(den, dens, den_sem)
@@ -145,35 +145,68 @@
         cp.start()
         zcopies.append(cp)
 
+    def transfer(source, target, send_sem, recv_sem, dx, dy):
+        cp = pltpu.make_async_remote_copy(
+            src_ref=source,
+            dst_ref=target,
+            send_sem=send_sem,
+            recv_sem=recv_sem,
+            device_id=near(dx, dy, 0),
+            device_id_type=MESH,
+        )
+        cp.start()
+        return cp
+
     third = lane // h
 
-    def gather_faces(rows, fresh):
-        @pl.loop(0, count)
-        def _(i):
-            for t in range(tiles):
-                span = slice(t * SUB, (t + 1) * SUB)
-                if fresh:
-                    head = jnp.zeros((SUB, nx), jnp.float32)
-                    tail = head
-                else:
-                    head, tail = raw[i, 0, span, :], raw[i, 1, span, :]
-                for z in rows:
-                    v = pltpu.roll(held[i, z, span, :], h * z + h, 1)
-                    head = jnp.where(third == z + 1, v, head)
-                    tail = jnp.where(third == z, v, tail)
-                raw[i, 0, span, :] = head
-                raw[i, 1, span, :] = tail
-
-    gather_faces(range(h, nz + h), True)
-
-    for p in range(h, SUB):
-        yc[p * zp:(p + 1) * zp, :] = jnp.zeros((zp, nx), jnp.float32)
-        mirror = 2 * SUB - 1 - p
-        yc[mirror * zp:(mirror + 1) * zp, :] = jnp.zeros((zp, nx), jnp.float32)
+    def gather_x(i, t, rows, head, tail):
+        span = slice(t * SUB, (t + 1) * SUB)
+        for z in rows:
+            v = pltpu.roll(held[i, z, span, :], h * z + h, 1)
+            head = jnp.where(third == z + 1, v, head)
+            tail = jnp.where(third == z, v, tail)
+        raw[i, 0, span, :] = head
+        raw[i, 1, span, :] = tail
+
+    def gather_y(i, rows):
+        for z in rows:
+            for k, t in enumerate((0, tiles - 1)):
+                yraw[i, pl.ds(k * SUB * zp + (z - h) % zp, SUB, stride=zp), :] = held[
+                    i, z, t * SUB:(t + 1) * SUB, :
+                ]
+
+    inner, outer = range(h, nz + h), (*range(h), *range(nz + h, ze))
+
+    @pl.loop(0, count)
+    def _(i):
+        zero = jnp.zeros((SUB, nx), jnp.float32)
+        for t in range(tiles):
+            gather_x(i, t, inner, zero, zero)
 
     for cp in zcopies:
         cp.wait()
-    gather_faces((*range(h), *range(nz + h, ze)), False)
+    for t in (0, tiles - 1, *range(1, tiles - 1)):
+        span = slice(t * SUB, (t + 1) * SUB)
+        for i in range(count):
+            gather_x(i, t, outer, raw[i, 0, span, :], raw[i, 1, span, :])
+    corners = []
+    for k, dx in enumerate((-1, 1)):
+        for end, (start, dy) in enumerate(((ny - SUB, 1), (0, -1))):
+            corners.append(
+                transfer(
+                    raw.at[:, k, pl.ds(start, SUB)], cland.at[1 - k, end],
+                    csend.at[k, end], crecv.at[k, end], dx, dy,
+                )
+            )
+
+    @pl.loop(0, count)
+    def _(i):
+        gather_y(i, range(ze))
+
+    for p in range(h, SUB):
+        mirror = 2 * SUB - 1 - p
+        yc[p * zp:(p + 1) * zp, :] = jnp.zeros((zp, nx), jnp.float32)
+        yc[mirror * zp:(mirror + 1) * zp, :] = jnp.zeros((zp, nx), jnp.float32)
 
     for k, (dx, dy, dz) in enumerate(offsets):
         source = (gx[-dx % cx] * cy + gy[-dy % cy]) * cz + gz[-dz % cz]
@@ -195,76 +228,55 @@
             b[i] = b[i] - f * b[k]
     solved = [None] * count
     for k in reversed(range(count)):
-        s = b[k]
-        for j in range(k + 1, count):
-            s = s - g[k, j] * solved[j]
-        solved[k] = s * inv[k]
+        solved[k] = b[k] * inv[k]
+        for i in range(k):
+            b[i] = b[i] - g[i, k] * solved[k]
     norm = solved[0]
     for k in range(1, count):
         norm = norm + solved[k]
     weights = [s / norm for s in solved]
 
+    def blend(parts):
+        s = weights[0] * parts(0)
+        for i in range(1, count):
+            s = s + weights[i] * parts(i)
+        return s
+
+    def combine_face(k):
+        for p in range(h):
+            source = (k * SUB + (p if k == 0 else SUB - 1 - p)) * zp
+            for r in range(0, zp, SUB):
+                ybuf[k, p * zp + r:p * zp + r + SUB, :] = blend(
+                    lambda i: yraw[i, source + r:source + r + SUB, :]
+                )
+
+    def send_y(k, dy):
+        message = pl.ds(0, h * zp - SUB)
+        return transfer(
+            ybuf.at[k, message], yland.at[1 - k, message], ysend.at[k], yrecv.at[k], 0, dy
+        )
+
+    combine_face(1)
+    ycopies = [send_y(1, 1)]
     for k in range(2):
         for t in range(tiles):
             span = slice(t * SUB, (t + 1) * SUB)
-            s = weights[0] * raw[0, k, span, :]
-            for i in range(1, count):
-                s = s + weights[i] * raw[i, k, span, :]
-            pack[k, span, :] = s
-
-    copies = []
-
-    def send(source, target, send_sem, recv_sem, dx, dy):
-        cp = pltpu.make_async_remote_copy(
-            src_ref=source,
-            dst_ref=target,
-            send_sem=send_sem,
-            recv_sem=recv_sem,
-            device_id=near(dx, dy, 0),
-            device_id_type=MESH,
-        )
-        cp.start()
-        copies.append(cp)
-
-    for k, dx in enumerate((-1, 1)):
-        side = land.at[1 - k]
-        send(
-            pack.at[k, pl.ds(ny - SUB, SUB)], side.at[pl.ds(0, SUB)],
-            csend.at[k, 0], crecv.at[k, 0], dx, 1,
-        )
-        send(
-            pack.at[k, pl.ds(0, SUB)], side.at[pl.ds(ny + SUB, SUB)],
-            csend.at[k, 1], crecv.at[k, 1], dx, -1,
-        )
-    for k, dx in enumerate((-1, 1)):
-        send(pack.at[k], land.at[1 - k, pl.ds(SUB, ny)], xsend.at[k], xrecv.at[k], dx, 0)
-
-    def combine(z, t):
-        span = slice(t * SUB, (t + 1) * SUB)
-        s = weights[0] * held[0, z, span, :]
-        for i in range(1, count):
-            s = s + weights[i] * held[i, z, span, :]
-        comb[z, span, :] = s
-        return s
+            pack[k, span, :] = blend(lambda i: raw[i, k, span, :])
+    combine_face(0)
+
+    xcopies = [
+        transfer(pack.at[k], land.at[1 - k, pl.ds(SUB, ny)], xsend.at[k], xrecv.at[k], dx, 0)
+        for k, dx in enumerate((-1, 1))
+    ]
+    ycopies.append(send_y(0, -1))
 
     @pl.loop(0, ze // 2)
     def _(half):
         for r in range(2):
             z = half * 2 + r
-            for k, t in enumerate((0, tiles - 1)):
-                ybuf[pl.ds(k * SUB * zp + z, SUB, stride=zp), :] = combine(z, t)
-
-    for k, (start, dy) in enumerate(((0, -1), ((2 * SUB - h) * zp, 1))):
-        send(
-            ybuf.at[pl.ds(start, h * zp)], yland.at[1 - k],
-            ysend.at[k], yrecv.at[k], 0, dy,
-        )
-
-    @pl.loop(0, ze // 2)
-    def _(half):
-        for r in range(2):
-            for t in range(1, tiles - 1):
-                combine(half * 2 + r, t)
+            for t in range(tiles):
+                span = slice(t * SUB, (t + 1) * SUB)
+                comb[z, span, :] = blend(lambda i: held[i, z, span, :])
 
     row = jnp.zeros((SUB, nx), jnp.float32)
     for k in range(count):
@@ -312,13 +324,7 @@
         u = keep * v + step * (rhs[z] + total)
         for t in range(tiles):
             span = slice(t * SUB, (t + 1) * SUB)
-            s = weights[0] * dens[0, z - h, span, :]
-            for i in range(1, count):
-                s = s + weights[i] * dens[i, z - h, span, :]
-            base[z - h, span, :] = s + u[span, :]
-
-    for cp in copies:
-        cp.wait()
+            base[z - h, span, :] = blend(lambda i: dens[i, z - h, span, :]) + u[span, :]
 
     _, c1, c2, c3 = neighbour_polynomial()
 
@@ -334,6 +340,14 @@
     def plane_sum(d):
         total = pltpu.roll(d, h, 1) + pltpu.roll(d, nx - h, 1)
         return total + (pltpu.roll(d, 1, 0) + pltpu.roll(d, wide - 1, 0))
+
+    for cp in corners:
+        cp.wait()
+    for s in range(2):
+        land[s, :SUB, :] = blend(lambda i: cland[s, 0, i])
+        land[s, ny + SUB:, :] = blend(lambda i: cland[s, 1, i])
+    for cp in xcopies:
+        cp.wait()
 
     sides = []
     for s in range(2):
@@ -356,6 +370,17 @@
     xc[0] = jnp.where(even, sides[1], sides[0])
     xc[1] = jnp.where(even, sides[0], sides[1])
 
+    edge = (lane < h) | (lane >= nx - h)
+    for z in range(nz):
+        e = z + h
+        for t in range(tiles):
+            span = slice(t * SUB, (t + 1) * SUB)
+            v = pltpu.roll(xc[e % 2, span, :], (-(h * e + h)) % nx, 1)
+            base[z, span, :] = base[z, span, :] + jnp.where(edge, v, 0.0)
+
+    for cp in ycopies:
+        cp.wait()
+
     along = lax.broadcasted_iota(jnp.int32, (zp, nx), 1)
     at_first, at_last = along == 0, along == nx - 1
 
@@ -365,58 +390,53 @@
         return total + (pltpu.roll(d, 1, 0) + pltpu.roll(d, zp - 1, 0))
 
     for s in range(2):
-        ds = []
-        for k in range(h):
-            p = h - 1 - k if s == 0 else k
-            q = 2 * SUB - 1 - k if s == 0 else k
-            ds.append(yland[s, p * zp:(p + 1) * zp, :] - ybuf[q * zp:(q + 1) * zp, :])
-        m = face_sum(ds[0])
-        mm = face_sum(m) + jnp.where(at_first | at_last, ds[0], 0.0)
-        near_1, near_2 = by_distance(ds[0], m, mm)
+        d1, d2 = (
+            yland[s, k * zp:(k + 1) * zp, :] - ybuf[1 - s, k * zp:(k + 1) * zp, :]
+            for k in range(2)
+        )
+        d3 = yland[s, 2 * zp:2 * zp + nz, :] - ybuf[1 - s, 2 * zp:2 * zp + nz, :]
+        m = face_sum(d1)
+        mm = face_sum(m) + jnp.where(at_first | at_last, d1, 0.0)
+        near_1, near_2 = by_distance(d1[:nz], m[:nz], mm[:nz])
         rows = [
-            near_1 + (c2 * ds[1] + (3.0 * c3) * face_sum(ds[1])) + c3 * ds[2],
-            near_2 + c3 * ds[1],
-            c3 * ds[0],
+            near_1 + (c2 * d2 + (3.0 * c3) * face_sum(d2))[:nz] + c3 * d3,
+            near_2 + c3 * d2[:nz],
+            c3 * d1[:nz],
         ]
         for j, r in enumerate(rows):
             p = j if s == 0 else 2 * SUB - 1 - j
-            yc[p * zp:(p + 1) * zp, :] = r
+            yc[p * zp:p * zp + nz, :] = r
 
     for k in range(len(offsets)):
         gram_copy(k, me).wait_send()
 
 
-def finish(base, xc, yc, weights, out, wout, stage, sem, wsem):
+def finish(base, yc, weights, out, wout, stage, sem, wsem):
     nz, ny, nx = base.shape
-    h = SWEEPS
     zp = yc.shape[0] // (2 * SUB)
-    tiles = ny // SUB
-    pieces = sem.shape[0]
+    pieces = sem.shape[0] - 1
     per = nz // pieces
-    wcopy = pltpu.make_async_copy(weights, wout, wsem)
-    wcopy.start()
-    lane = lax.broadcasted_iota(jnp.int32, (SUB, nx), 1)
-    edge = (lane < h) | (lane >= nx - h)
     copies = []
-    for c in range(pieces):
-        for z in range(c * per, (c + 1) * per):
-            e = z + h
-            for t in range(tiles):
-                span = slice(t * SUB, (t + 1) * SUB)
-                v = pltpu.roll(xc[e % 2, span, :], (-(h * e + h)) % nx, 1)
-                v = base[z, span, :] + jnp.where(edge, v, 0.0)
-                if t == 0:
-                    v = v + yc[pl.ds(e, SUB, stride=zp), :]
-                if t == tiles - 1:
-                    v = v + yc[pl.ds(SUB * zp + e, SUB, stride=zp), :]
-                stage[z, span, :] = v
-        part = pl.ds(c * per, per)
-        cp = pltpu.make_async_copy(stage.at[part], out.at[part], sem.at[c])
+
+    def store(source, target, sem):
+        cp = pltpu.make_async_copy(source, target, sem)
         cp.start()
         copies.append(cp)
+
+    store(weights, wout, wsem)
+    if ny > 2 * SUB:
+        middle = pl.ds(SUB, ny - 2 * SUB)
+        store(base.at[:, middle], out.at[:, middle], sem.at[pieces, 0])
+    for c in range(pieces):
+        part = pl.ds(c * per, per)
+        for k, start in enumerate((0, ny - SUB)):
+            for z in range(c * per, (c + 1) * per):
+                stage[k, z] = base[z, start:start + SUB, :] + yc[
+                    pl.ds(k * SUB * zp + z, SUB, stride=zp), :
+                ]
+            store(stage.at[k, part], out.at[part, pl.ds(start, SUB)], sem.at[c, k])
     for cp in copies:
         cp.wait()
-    wcopy.wait()
 
 
 def on_device(counts, densities, residuals):
@@ -439,12 +459,11 @@
         functools.partial(kernel, counts, dims, chunks),
         out_shape=(
             pltpu.VMEM((nz, ny, nx), f32),
-            pltpu.VMEM((2, ny, nx), f32),
             pltpu.VMEM((2 * SUB * zp, nx), f32),
             pltpu.VMEM((1, count), f32),
         ),
         in_specs=[any_spec, any_spec],
-        out_specs=(vmem, vmem, vmem, vmem),
+        out_specs=(vmem, vmem, vmem),
         scratch_shapes=[
             pltpu.VMEM((count, ze, ny, nx), f32),
             pltpu.VMEM(dims, f32),
@@ -453,8 +472,11 @@
             pltpu.VMEM((count, 2, ny, nx), f32),
             pltpu.VMEM((2, ny, nx), f32),
             pltpu.VMEM((2, ny + 2 * SUB, nx), f32),
-            pltpu.VMEM((2 * SUB * zp, nx), f32),
+            pltpu.VMEM((2, 2, count, SUB, nx), f32),
+            pltpu.VMEM((count, 2 * SUB * zp, nx), f32),
             pltpu.VMEM((2, h * zp, nx), f32),
+            pltpu.VMEM((2, h * zp, nx), f32),
+            pltpu.VMEM((2, ny, nx), f32),
             dma((chunks,)), dma(()), dma((n,)), dma((n,)),
             dma((2,)), dma((2,)), dma((2,)), dma((2,)), dma((2,)), dma((2,)), dma((2, 2)), dma((2, 2)),
         ],
@@ -468,9 +490,9 @@
             jax.ShapeDtypeStruct((nz, ny, nx), f32),
             jax.ShapeDtypeStruct((1, count), f32),
         ),
-        in_specs=[vmem, vmem, vmem, vmem],
+        in_specs=[vmem, vmem, vmem],
         out_specs=(any_spec, any_spec),
-        scratch_shapes=[pltpu.VMEM((nz, ny, nx), f32), dma((8,)), dma(())],
+        scratch_shapes=[pltpu.VMEM((2, nz, SUB, nx), f32), dma((5, 2)), dma(())],
         compiler_params=pltpu.CompilerParams(vmem_limit_bytes=4 * 1024 * 1024),
     )(*parts)
     return new_density, weights.reshape(count)

time: 19.6 us -> 18.7 us (0.954)
  Pallas kernels: 18.8 us -> 17.9 us
    pallas_call x1, Pallas kernels: 17.9 us -> 17 us  [on_device(): pl.pallas_call(functools.partial(kernel, counts, dims, chunks), out_shape...]
where the time goes in v2:
time: 18.7 us; the launch traced here: 18.5 us
  Pallas kernels  17.9 us (96%)
  between operations  0.64 us (3%)
    pallas_call x1, Pallas kernels, on_device(): pl.pallas_call(functools.partial(kernel, counts, dims, chunks), out_shape...  17 us
    pallas_call x1, Pallas kernels, on_device(): pl.pallas_call(finish, out_shape=(jax.ShapeDtypeStruct((nz, ny, nx), f32)...  0.88 us

profile of v2, /device:TPU:0, one launch (start us, length us, event | category | flops | bytes accessed | tf_op | source)
XLA Modules:
  0.0 18.5 jit_solution(2506214494315564583)
XLA Ops:
  0.6 17.0 %shard_map.41 = (f32[32,32,128]{2,1,0:T(8,128)S(1)}, f32[640,128]{1,0:T(8,128)S(1)}, f32[1,7]{1,0:T(1,128)S(1)}) custom-call(f32[7,32,32,128]{3,2,1,0:T(8,128)} %res.1, f32[7,32,32,128]{3,2,1,0:T(8,128)} %den.1), custom_call_target="tpu_custom_call" | custom-call | tf_op jit(solution)/shard_map/pallas_call | solution.py:458
  17.6 0.9 %shard_map.42 = (f32[32,32,128]{2,1,0:T(8,128)}, f32[1,7]{1,0:T(1,128)}) custom-call(f32[32,32,128]{2,1,0:T(8,128)S(1)} %get-tuple-element.7.base, f32[640,128]{1,0:T(8,128)S(1)} %get-tuple-element.8.yc, f32[1,7]{1,0:T(1,128)S(1)} %get-tuple-element.9.weights), custom_call_target="tpu_custom_call" | custom-call | tf_op jit(solution)/shard_map/pallas_call | solution.py:487

commit v3 on v2

--- a/solution.py
+++ b/solution.py
@@ -50,7 +50,7 @@
 def kernel(
     counts, dims, chunks,
     res, den, base, yc, wout,
-    held, dens, slots, comb, rhs, it, raw, pack, land, cland, yraw, ybuf, yland, xc,
+    held, dens, slots, comb, rhs, it, raw, pack, land, cpack, cland, yraw, ybuf, yland, xc,
     in_sem, den_sem, gsend, grecv, zsend, zrecv, ysend, yrecv, xsend, xrecv, csend, crecv,
 ):
     count, nz, ny, nx = dims
@@ -70,6 +70,15 @@
             lax.rem(iz + dz + cz, cz),
         )
 
+    per = nz // chunks
+    loads = []
+    for c in range(chunks):
+        cp = pltpu.make_async_copy(
+            res.at[:, pl.ds(c * per, per)], held.at[:, pl.ds(h + c * per, per)], in_sem.at[c]
+        )
+        cp.start()
+        loads.append(cp)
+
     barrier = pltpu.get_barrier_semaphore()
 
     offsets = [
@@ -84,15 +93,6 @@
             barrier, inc=1, device_id=(gx[dx], gy[dy], gz[dz]), device_id_type=MESH
         )
 
-    per = nz // chunks
-    loads = []
-    for c in range(chunks):
-        cp = pltpu.make_async_copy(
-            res.at[:, pl.ds(c * per, per)], held.at[:, pl.ds(h + c * per, per)], in_sem.at[c]
-        )
-        cp.start()
-        loads.append(cp)
-
     pairs = [(i, j) for i in range(count) for j in range(i, count)]
     accs = tuple(jnp.zeros((SUB, nx), jnp.float32) for _ in pairs)
     den_load = pltpu.make_async_copy(den, dens, den_sem)
@@ -189,12 +189,22 @@
         span = slice(t * SUB, (t + 1) * SUB)
         for i in range(count):
             gather_x(i, t, outer, raw[i, 0, span, :], raw[i, 1, span, :])
+
     corners = []
-    for k, dx in enumerate((-1, 1)):
-        for end, (start, dy) in enumerate(((ny - SUB, 1), (0, -1))):
+    flat_raw = raw.reshape(count * 2 * ny, nx)
+    turn = (2, nx - 2)
+    far = tuple(
+        lax.broadcasted_iota(jnp.int32, (count, nx), 1) % h == c for c in (h - 1, 0)
+    )
+    for end, (first, second, dy) in enumerate(((ny - 1, ny - 2, 1), (0, 1, -1))):
+        for k, dx in enumerate((-1, 1)):
+            one, two = (
+                flat_raw[pl.ds(k * ny + y, count, stride=2 * ny), :] for y in (first, second)
+            )
+            cpack[k, end] = jnp.where(far[k], pltpu.roll(two, turn[k], 1), one)
             corners.append(
                 transfer(
-                    raw.at[:, k, pl.ds(start, SUB)], cland.at[1 - k, end],
+                    cpack.at[k, end], cland.at[1 - k, end],
                     csend.at[k, end], crecv.at[k, end], dx, dy,
                 )
             )
@@ -343,9 +353,13 @@
 
     for cp in corners:
         cp.wait()
+    sub = lax.broadcasted_iota(jnp.int32, (SUB, nx), 0)
     for s in range(2):
-        land[s, :SUB, :] = blend(lambda i: cland[s, 0, i])
-        land[s, ny + SUB:, :] = blend(lambda i: cland[s, 1, i])
+        for end, (start, nearest) in enumerate(((0, SUB - 1), (ny + SUB, 0))):
+            found = blend(lambda i: jnp.broadcast_to(cland[s, end, i:i + 1, :], (SUB, nx)))
+            land[s, start:start + SUB, :] = jnp.where(
+                sub == nearest, found, pltpu.roll(found, turn[s], 1)
+            )
     for cp in xcopies:
         cp.wait()
 
@@ -472,7 +486,8 @@
             pltpu.VMEM((count, 2, ny, nx), f32),
             pltpu.VMEM((2, ny, nx), f32),
             pltpu.VMEM((2, ny + 2 * SUB, nx), f32),
-            pltpu.VMEM((2, 2, count, SUB, nx), f32),
+            pltpu.VMEM((2, 2, count, nx), f32),
+            pltpu.VMEM((2, 2, count, nx), f32),
             pltpu.VMEM((count, 2 * SUB * zp, nx), f32),
             pltpu.VMEM((2, h * zp, nx), f32),
             pltpu.VMEM((2, h * zp, nx), f32),

time: 18.7 us -> 18.2 us (0.973)
  Pallas kernels: 17.9 us -> 17.4 us
    pallas_call x1, Pallas kernels: 17 us -> 16.5 us  [on_device(): pl.pallas_call(functools.partial(kernel, counts, dims, chunks), out_shape...]
where the time goes in v3:
time: 18.2 us; the launch traced here: 18 us
  Pallas kernels  17.4 us (96%)
  between operations  0.64 us (4%)
    pallas_call x1, Pallas kernels, on_device(): pl.pallas_call(functools.partial(kernel, counts, dims, chunks), out_shape...  16.5 us
    pallas_call x1, Pallas kernels, on_device(): pl.pallas_call(finish, out_shape=(jax.ShapeDtypeStruct((nz, ny, nx), f32)...  0.88 us

profile of v3, /device:TPU:0, one launch (start us, length us, event | category | flops | bytes accessed | tf_op | source)
XLA Modules:
  0.0 18.0 jit_solution(14608109364425812593)
XLA Ops:
  0.6 16.5 %shard_map.41 = (f32[32,32,128]{2,1,0:T(8,128)S(1)}, f32[640,128]{1,0:T(8,128)S(1)}, f32[1,7]{1,0:T(1,128)S(1)}) custom-call(f32[7,32,32,128]{3,2,1,0:T(8,128)} %res.1, f32[7,32,32,128]{3,2,1,0:T(8,128)} %den.1), custom_call_target="tpu_custom_call" | custom-call | tf_op jit(solution)/shard_map/pallas_call | solution.py:472
  17.2 0.9 %shard_map.42 = (f32[32,32,128]{2,1,0:T(8,128)}, f32[1,7]{1,0:T(1,128)}) custom-call(f32[32,32,128]{2,1,0:T(8,128)S(1)} %get-tuple-element.7.base, f32[640,128]{1,0:T(8,128)S(1)} %get-tuple-element.8.yc, f32[1,7]{1,0:T(1,128)S(1)} %get-tuple-element.9.weights), custom_call_target="tpu_custom_call" | custom-call | tf_op jit(solution)/shard_map/pallas_call | solution.py:502

commit v4 on v3

--- a/solution.py
+++ b/solution.py
@@ -11,7 +11,7 @@
 MESH = pl.DeviceIdType.MESH
 SWEEPS = 3
 SUB = 8
-UNROLL = 4
+UNROLL = 12
 shift_value = 0.15
 mix_amount = 0.7
 AXES = ("gx", "gy", "gz")
@@ -118,32 +118,40 @@
 
     pl.semaphore_wait(barrier, total_devices - 1)
 
-    def gram_copy(k, slot):
+    def gram_copy(k):
         dx, dy, dz = offsets[k]
         return pltpu.make_async_remote_copy(
             src_ref=slots.at[me],
-            dst_ref=slots.at[slot],
-            send_sem=gsend.at[k],
-            recv_sem=grecv.at[k],
+            dst_ref=slots.at[me],
+            send_sem=gsend,
+            recv_sem=grecv,
             device_id=(gx[dx], gy[dy], gz[dz]),
             device_id_type=MESH,
         )
 
     for k in range(len(offsets)):
-        gram_copy(k, me).start()
-
-    zcopies = []
+        gram_copy(k).start()
+
+    def all_of(ref, send_sem, recv_sem):
+        return pltpu.make_async_remote_copy(
+            src_ref=ref,
+            dst_ref=ref,
+            send_sem=send_sem,
+            recv_sem=recv_sem,
+            device_id=near(0, 0, 1),
+            device_id_type=MESH,
+        )
+
     for k, (start, dest, dz) in enumerate(((h, nz + h, -1), (nz, 0, 1))):
         cp = pltpu.make_async_remote_copy(
             src_ref=held.at[:, pl.ds(start, h)],
             dst_ref=held.at[:, pl.ds(dest, h)],
-            send_sem=zsend.at[k],
-            recv_sem=zrecv.at[k],
+            send_sem=zsend,
+            recv_sem=zrecv,
             device_id=near(0, 0, dz),
             device_id_type=MESH,
         )
         cp.start()
-        zcopies.append(cp)
 
     def transfer(source, target, send_sem, recv_sem, dx, dy):
         cp = pltpu.make_async_remote_copy(
@@ -155,7 +163,6 @@
             device_id_type=MESH,
         )
         cp.start()
-        return cp
 
     third = lane // h
 
@@ -183,14 +190,12 @@
         for t in range(tiles):
             gather_x(i, t, inner, zero, zero)
 
-    for cp in zcopies:
-        cp.wait()
+    all_of(held.at[:, pl.ds(0, 2 * h)], zsend, zrecv).wait()
     for t in (0, tiles - 1, *range(1, tiles - 1)):
         span = slice(t * SUB, (t + 1) * SUB)
         for i in range(count):
             gather_x(i, t, outer, raw[i, 0, span, :], raw[i, 1, span, :])
 
-    corners = []
     flat_raw = raw.reshape(count * 2 * ny, nx)
     turn = (2, nx - 2)
     far = tuple(
@@ -202,12 +207,7 @@
                 flat_raw[pl.ds(k * ny + y, count, stride=2 * ny), :] for y in (first, second)
             )
             cpack[k, end] = jnp.where(far[k], pltpu.roll(two, turn[k], 1), one)
-            corners.append(
-                transfer(
-                    cpack.at[k, end], cland.at[1 - k, end],
-                    csend.at[k, end], crecv.at[k, end], dx, dy,
-                )
-            )
+            transfer(cpack.at[k, end], cland.at[1 - k, end], csend, crecv, dx, dy)
 
     @pl.loop(0, count)
     def _(i):
@@ -218,9 +218,8 @@
         yc[p * zp:(p + 1) * zp, :] = jnp.zeros((zp, nx), jnp.float32)
         yc[mirror * zp:(mirror + 1) * zp, :] = jnp.zeros((zp, nx), jnp.float32)
 
-    for k, (dx, dy, dz) in enumerate(offsets):
-        source = (gx[-dx % cx] * cy + gy[-dy % cy]) * cz + gz[-dz % cz]
-        gram_copy(k, source).wait_recv()
+    gram_all = all_of(slots.at[pl.ds(0, total_devices - 1)], gsend, grecv)
+    gram_all.wait_recv()
 
     total = jnp.sum(slots[...], axis=0)
 
@@ -260,25 +259,22 @@
                     lambda i: yraw[i, source + r:source + r + SUB, :]
                 )
 
+    message = pl.ds(0, h * zp - SUB)
+
     def send_y(k, dy):
-        message = pl.ds(0, h * zp - SUB)
-        return transfer(
-            ybuf.at[k, message], yland.at[1 - k, message], ysend.at[k], yrecv.at[k], 0, dy
-        )
+        transfer(ybuf.at[k, message], yland.at[1 - k, message], ysend, yrecv, 0, dy)
 
     combine_face(1)
-    ycopies = [send_y(1, 1)]
+    send_y(1, 1)
     for k in range(2):
         for t in range(tiles):
             span = slice(t * SUB, (t + 1) * SUB)
             pack[k, span, :] = blend(lambda i: raw[i, k, span, :])
     combine_face(0)
 
-    xcopies = [
-        transfer(pack.at[k], land.at[1 - k, pl.ds(SUB, ny)], xsend.at[k], xrecv.at[k], dx, 0)
-        for k, dx in enumerate((-1, 1))
-    ]
-    ycopies.append(send_y(0, -1))
+    for k, dx in enumerate((-1, 1)):
+        transfer(pack.at[k], land.at[1 - k, pl.ds(SUB, ny)], xsend, xrecv, dx, 0)
+    send_y(0, -1)
 
     @pl.loop(0, ze // 2)
     def _(half):
@@ -351,8 +347,7 @@
         total = pltpu.roll(d, h, 1) + pltpu.roll(d, nx - h, 1)
         return total + (pltpu.roll(d, 1, 0) + pltpu.roll(d, wide - 1, 0))
 
-    for cp in corners:
-        cp.wait()
+    all_of(cland, csend, crecv).wait()
     sub = lax.broadcasted_iota(jnp.int32, (SUB, nx), 0)
     for s in range(2):
         for end, (start, nearest) in enumerate(((0, SUB - 1), (ny + SUB, 0))):
@@ -360,8 +355,7 @@
             land[s, start:start + SUB, :] = jnp.where(
                 sub == nearest, found, pltpu.roll(found, turn[s], 1)
             )
-    for cp in xcopies:
-        cp.wait()
+    all_of(land.at[:, pl.ds(SUB, ny)], xsend, xrecv).wait()
 
     sides = []
     for s in range(2):
@@ -392,8 +386,7 @@
             v = pltpu.roll(xc[e % 2, span, :], (-(h * e + h)) % nx, 1)
             base[z, span, :] = base[z, span, :] + jnp.where(edge, v, 0.0)
 
-    for cp in ycopies:
-        cp.wait()
+    all_of(yland.at[:, message], ysend, yrecv).wait()
 
     along = lax.broadcasted_iota(jnp.int32, (zp, nx), 1)
     at_first, at_last = along == 0, along == nx - 1
@@ -421,26 +414,23 @@
             p = j if s == 0 else 2 * SUB - 1 - j
             yc[p * zp:p * zp + nz, :] = r
 
-    for k in range(len(offsets)):
-        gram_copy(k, me).wait_send()
+    gram_all.wait_send()
 
 
 def finish(base, yc, weights, out, wout, stage, sem, wsem):
     nz, ny, nx = base.shape
     zp = yc.shape[0] // (2 * SUB)
-    pieces = sem.shape[0] - 1
+    pieces = 4
     per = nz // pieces
-    copies = []
-
-    def store(source, target, sem):
-        cp = pltpu.make_async_copy(source, target, sem)
-        cp.start()
-        copies.append(cp)
-
-    store(weights, wout, wsem)
+
+    def store(source, target):
+        pltpu.make_async_copy(source, target, sem).start()
+
+    wcopy = pltpu.make_async_copy(weights, wout, wsem)
+    wcopy.start()
     if ny > 2 * SUB:
         middle = pl.ds(SUB, ny - 2 * SUB)
-        store(base.at[:, middle], out.at[:, middle], sem.at[pieces, 0])
+        store(base.at[:, middle], out.at[:, middle])
     for c in range(pieces):
         part = pl.ds(c * per, per)
         for k, start in enumerate((0, ny - SUB)):
@@ -448,9 +438,9 @@
                 stage[k, z] = base[z, start:start + SUB, :] + yc[
                     pl.ds(k * SUB * zp + z, SUB, stride=zp), :
                 ]
-            store(stage.at[k, part], out.at[part, pl.ds(start, SUB)], sem.at[c, k])
-    for cp in copies:
-        cp.wait()
+            store(stage.at[k, part], out.at[part, pl.ds(start, SUB)])
+    pltpu.make_async_copy(base, out, sem).wait()
+    wcopy.wait()
 
 
 def on_device(counts, densities, residuals):
@@ -492,8 +482,7 @@
             pltpu.VMEM((2, h * zp, nx), f32),
             pltpu.VMEM((2, h * zp, nx), f32),
             pltpu.VMEM((2, ny, nx), f32),
-            dma((chunks,)), dma(()), dma((n,)), dma((n,)),
-            dma((2,)), dma((2,)), dma((2,)), dma((2,)), dma((2,)), dma((2,)), dma((2, 2)), dma((2, 2)),
+            dma((chunks,)), *(dma(()) for _ in range(11)),
         ],
         compiler_params=pltpu.CompilerParams(
             collective_id=0, has_side_effects=True, vmem_limit_bytes=56 * 1024 * 1024
@@ -507,7 +496,7 @@
         ),
         in_specs=[vmem, vmem, vmem],
         out_specs=(any_spec, any_spec),
-        scratch_shapes=[pltpu.VMEM((2, nz, SUB, nx), f32), dma((5, 2)), dma(())],
+        scratch_shapes=[pltpu.VMEM((2, nz, SUB, nx), f32), dma(()), dma(())],
         compiler_params=pltpu.CompilerParams(vmem_limit_bytes=4 * 1024 * 1024),
     )(*parts)
     return new_density, weights.reshape(count)

time: 18.2 us -> 17.4 us (0.956)
  Pallas kernels: 17.4 us -> 16.6 us
    pallas_call x1, Pallas kernels: 16.5 us -> 15.8 us  [on_device(): pl.pallas_call(functools.partial(kernel, counts, dims, chunks), out_shape...]
where the time goes in v4:
time: 17.4 us; the launch traced here: 17.2 us
  Pallas kernels  16.6 us (95%)
  between operations  0.64 us (4%)
    pallas_call x1, Pallas kernels, on_device(): pl.pallas_call(functools.partial(kernel, counts, dims, chunks), out_shape...  15.8 us
    pallas_call x1, Pallas kernels, on_device(): pl.pallas_call(finish, out_shape=(jax.ShapeDtypeStruct((nz, ny, nx), f32)...  0.8 us

profile of v4, /device:TPU:0, one launch (start us, length us, event | category | flops | bytes accessed | tf_op | source)
XLA Modules:
  0.0 17.2 jit_solution(11120365350009895224)
XLA Ops:
  0.6 15.8 %shard_map.41 = (f32[32,32,128]{2,1,0:T(8,128)S(1)}, f32[640,128]{1,0:T(8,128)S(1)}, f32[1,7]{1,0:T(1,128)S(1)}) custom-call(f32[7,32,32,128]{3,2,1,0:T(8,128)} %res.1, f32[7,32,32,128]{3,2,1,0:T(8,128)} %den.1), custom_call_target="tpu_custom_call" | custom-call | tf_op jit(solution)/shard_map/pallas_call | solution.py:462
  16.4 0.8 %shard_map.42 = (f32[32,32,128]{2,1,0:T(8,128)}, f32[1,7]{1,0:T(1,128)}) custom-call(f32[32,32,128]{2,1,0:T(8,128)S(1)} %get-tuple-element.7.base, f32[640,128]{1,0:T(8,128)S(1)} %get-tuple-element.8.yc, f32[1,7]{1,0:T(1,128)S(1)} %get-tuple-element.9.weights), custom_call_target="tpu_custom_call" | custom-call | tf_op jit(solution)/shard_map/pallas_call | solution.py:491

commit v5 on v4

--- a/solution.py
+++ b/solution.py
@@ -50,15 +50,16 @@
 def kernel(
     counts, dims, chunks,
     res, den, base, yc, wout,
-    held, dens, slots, comb, rhs, it, raw, pack, land, cpack, cland, yraw, ybuf, yland, xc,
-    in_sem, den_sem, gsend, grecv, zsend, zrecv, ysend, yrecv, xsend, xrecv, csend, crecv,
+    held, dens, slots, comb, rhs, it, raw, pack, land, cpack, cland,
+    yraw, ycon, ymate, ymix, ybuf, yland, xc,
+    in_sem, den_sem, sent, grecv, zrecv, mrecv, xrecv, yrecv,
 ):
     count, nz, ny, nx = dims
     cx, cy, cz = counts
     total_devices = cx * cy * cz
     h = SWEEPS
     ze = nz + 2 * h
-    zp = yland.shape[1] // h
+    zp = yraw.shape[1] // (2 * SUB)
     tiles = ny // SUB
     ix, iy, iz = (lax.axis_index(a) for a in AXES)
     me = (ix * cy + iy) * cz + iz
@@ -70,21 +71,22 @@
             lax.rem(iz + dz + cz, cz),
         )
 
-    per = nz // chunks
-    loads = []
-    for c in range(chunks):
+    loads, first = [], 0
+    for c, size in enumerate(chunks):
         cp = pltpu.make_async_copy(
-            res.at[:, pl.ds(c * per, per)], held.at[:, pl.ds(h + c * per, per)], in_sem.at[c]
+            res.at[:, pl.ds(first, size)], held.at[:, pl.ds(h + first, size)], in_sem.at[c]
         )
         cp.start()
-        loads.append(cp)
+        loads.append((cp, h + first, h + first + size))
+        first += size
 
     barrier = pltpu.get_barrier_semaphore()
 
     offsets = [
         (dx, dy, dz) for dx in range(cx) for dy in range(cy) for dz in range(cz) if dx or dy or dz
     ]
-    offsets.sort(key=lambda o: -sum(min(d, c - d) for d, c in zip(o, counts)))
+    order = [1, cy - 1, *range(2, cy - 1), 0]
+    offsets.sort(key=lambda o: (-(o[0] % 2), order.index(o[1])))
     gx = [lax.rem(ix + d, cx) for d in range(cx)]
     gy = [lax.rem(iy + d, cy) for d in range(cy)]
     gz = [lax.rem(iz + d, cz) for d in range(cz)]
@@ -96,9 +98,9 @@
     pairs = [(i, j) for i in range(count) for j in range(i, count)]
     accs = tuple(jnp.zeros((SUB, nx), jnp.float32) for _ in pairs)
     den_load = pltpu.make_async_copy(den, dens, den_sem)
-    for c in range(chunks):
-        loads[c].wait()
-        if c == chunks - 1:
+    for c, (load, start, stop) in enumerate(loads):
+        load.wait()
+        if c == len(loads) - 1:
             den_load.start()
 
         def gram_step(z, accs):
@@ -109,7 +111,7 @@
                     accs[p] = accs[p] + v[i] * v[j]
             return tuple(accs)
 
-        accs = lax.fori_loop(h + c * per, h + (c + 1) * per, gram_step, accs)
+        accs = lax.fori_loop(start, stop, gram_step, accs)
     lane = lax.broadcasted_iota(jnp.int32, (SUB, nx), 1)
     packed = jnp.zeros((SUB, nx), jnp.float32)
     for p in range(len(pairs)):
@@ -118,26 +120,28 @@
 
     pl.semaphore_wait(barrier, total_devices - 1)
 
-    def gram_copy(k):
-        dx, dy, dz = offsets[k]
+    def gram_copy(dx, dy, dz):
         return pltpu.make_async_remote_copy(
             src_ref=slots.at[me],
             dst_ref=slots.at[me],
-            send_sem=gsend,
+            send_sem=sent,
             recv_sem=grecv,
             device_id=(gx[dx], gy[dy], gz[dz]),
             device_id_type=MESH,
         )
 
-    for k in range(len(offsets)):
-        gram_copy(k).start()
-
-    def all_of(ref, send_sem, recv_sem):
+    for dx, dy, dz in sorted(offsets, key=lambda o: (-(o[0] % 2), order.index(-o[1] % cy))):
+        gram_copy(dx, dy, dz).start()
+
+    flat_held = held.reshape(count * ze * ny, nx)
+
+    def all_of(rows, sem):
+        part = flat_held.at[pl.ds(0, rows)]
         return pltpu.make_async_remote_copy(
-            src_ref=ref,
-            dst_ref=ref,
-            send_sem=send_sem,
-            recv_sem=recv_sem,
+            src_ref=part,
+            dst_ref=part,
+            send_sem=sem,
+            recv_sem=sem,
             device_id=near(0, 0, 1),
             device_id_type=MESH,
         )
@@ -146,23 +150,22 @@
         cp = pltpu.make_async_remote_copy(
             src_ref=held.at[:, pl.ds(start, h)],
             dst_ref=held.at[:, pl.ds(dest, h)],
-            send_sem=zsend,
+            send_sem=sent,
             recv_sem=zrecv,
             device_id=near(0, 0, dz),
             device_id_type=MESH,
         )
         cp.start()
 
-    def transfer(source, target, send_sem, recv_sem, dx, dy):
-        cp = pltpu.make_async_remote_copy(
+    def transfer(source, target, recv_sem, dx, dy, dz=0):
+        pltpu.make_async_remote_copy(
             src_ref=source,
             dst_ref=target,
-            send_sem=send_sem,
+            send_sem=sent,
             recv_sem=recv_sem,
-            device_id=near(dx, dy, 0),
+            device_id=near(dx, dy, dz),
             device_id_type=MESH,
-        )
-        cp.start()
+        ).start()
 
     third = lane // h
 
@@ -175,22 +178,67 @@
         raw[i, 0, span, :] = head
         raw[i, 1, span, :] = tail
 
-    def gather_y(i, rows):
+    def gather_y(i, k, rows):
+        start = k * (ny - SUB)
         for z in rows:
-            for k, t in enumerate((0, tiles - 1)):
-                yraw[i, pl.ds(k * SUB * zp + (z - h) % zp, SUB, stride=zp), :] = held[
-                    i, z, t * SUB:(t + 1) * SUB, :
-                ]
+            yraw[i, pl.ds(k * SUB * zp + (z - h) % zp, SUB, stride=zp), :] = held[
+                i, z, start:start + SUB, :
+            ]
 
     inner, outer = range(h, nz + h), (*range(h), *range(nz + h, ze))
 
     @pl.loop(0, count)
     def _(i):
+        gather_y(i, 1, inner)
         zero = jnp.zeros((SUB, nx), jnp.float32)
         for t in range(tiles):
             gather_x(i, t, inner, zero, zero)
 
-    all_of(held.at[:, pl.ds(0, 2 * h)], zsend, zrecv).wait()
+    all_of(2 * count * h * ny, zrecv).wait_recv()
+    for i in range(count):
+        gather_y(i, 1, outer)
+
+    _, c1, c2, c3 = neighbour_polynomial()
+
+    def by_distance(first, second, square):
+        near_by = (c1 + 3.0 * c3) * first + (2.0 * c2) * second + (3.0 * c3) * square
+        return near_by, c2 * first + (3.0 * c3) * second
+
+    along = lax.broadcasted_iota(jnp.int32, (zp, nx), 1)
+    at_first, at_last = along == 0, along == nx - 1
+
+    def face_sum(d):
+        total = jnp.where(at_first, 0.0, pltpu.roll(d, 1, 1))
+        total = total + jnp.where(at_last, 0.0, pltpu.roll(d, nx - 1, 1))
+        return total + (pltpu.roll(d, 1, 0) + pltpu.roll(d, zp - 1, 0))
+
+    def contribute(i, k):
+        d1, d2, d3 = (
+            yraw[i, p * zp:(p + 1) * zp, :]
+            for p in (range(h) if k == 0 else range(2 * SUB - 1, 2 * SUB - 1 - h, -1))
+        )
+        m = face_sum(d1)
+        mm = face_sum(m) + jnp.where(at_first | at_last, d1, 0.0)
+        near_1, near_2 = by_distance(d1[:nz], m[:nz], mm[:nz])
+        rows = [
+            near_1 + (c2 * d2 + (3.0 * c3) * face_sum(d2))[:nz] + c3 * d3[:nz],
+            near_2 + c3 * d2[:nz],
+            c3 * d1[:nz],
+        ]
+        for j, r in enumerate(rows):
+            q = j if k == 1 else h - 1 - j
+            ycon[k, i, q * nz:(q + 1) * nz, :] = r
+
+    for i in range(count):
+        contribute(i, 1)
+
+    odd = lax.rem(iz, 2) == 1
+    mate_rows = count * h * nz
+
+    @pl.when(jnp.logical_not(odd))
+    def _():
+        transfer(ycon.at[1], ymate, mrecv, 0, 0, 1)
+
     for t in (0, tiles - 1, *range(1, tiles - 1)):
         span = slice(t * SUB, (t + 1) * SUB)
         for i in range(count):
@@ -207,19 +255,25 @@
                 flat_raw[pl.ds(k * ny + y, count, stride=2 * ny), :] for y in (first, second)
             )
             cpack[k, end] = jnp.where(far[k], pltpu.roll(two, turn[k], 1), one)
-            transfer(cpack.at[k, end], cland.at[1 - k, end], csend, crecv, dx, dy)
+            transfer(cpack.at[k, end], cland.at[1 - k, end], xrecv, dx, dy)
 
     @pl.loop(0, count)
     def _(i):
-        gather_y(i, range(ze))
+        gather_y(i, 0, range(ze))
+
+    for i in range(count):
+        contribute(i, 0)
 
     for p in range(h, SUB):
         mirror = 2 * SUB - 1 - p
         yc[p * zp:(p + 1) * zp, :] = jnp.zeros((zp, nx), jnp.float32)
         yc[mirror * zp:(mirror + 1) * zp, :] = jnp.zeros((zp, nx), jnp.float32)
 
-    gram_all = all_of(slots.at[pl.ds(0, total_devices - 1)], gsend, grecv)
-    gram_all.wait_recv()
+    @pl.when(odd)
+    def _():
+        all_of(mate_rows, mrecv).wait_recv()
+
+    all_of(total_devices - 1, grecv).wait_recv()
 
     total = jnp.sum(slots[...], axis=0)
 
@@ -251,30 +305,33 @@
             s = s + weights[i] * parts(i)
         return s
 
-    def combine_face(k):
-        for p in range(h):
-            source = (k * SUB + (p if k == 0 else SUB - 1 - p)) * zp
-            for r in range(0, zp, SUB):
-                ybuf[k, p * zp + r:p * zp + r + SUB, :] = blend(
-                    lambda i: yraw[i, source + r:source + r + SUB, :]
-                )
-
-    message = pl.ds(0, h * zp - SUB)
-
-    def send_y(k, dy):
-        transfer(ybuf.at[k, message], yland.at[1 - k, message], ysend, yrecv, 0, dy)
-
-    combine_face(1)
-    send_y(1, 1)
+    message_rows = h * nz
+
+    def combine_face(target, source):
+        for r in range(0, message_rows, SUB):
+            target[r:r + SUB, :] = blend(lambda i: source[i, r:r + SUB, :])
+
+    @pl.when(odd)
+    def _():
+        combine_face(ymix, ymate)
+        transfer(ymix, yland.at[0], yrecv, 0, 1, -1)
+
     for k in range(2):
         for t in range(tiles):
             span = slice(t * SUB, (t + 1) * SUB)
             pack[k, span, :] = blend(lambda i: raw[i, k, span, :])
-    combine_face(0)
-
     for k, dx in enumerate((-1, 1)):
-        transfer(pack.at[k], land.at[1 - k, pl.ds(SUB, ny)], xsend, xrecv, dx, 0)
-    send_y(0, -1)
+        transfer(pack.at[k], land.at[1 - k, pl.ds(SUB, ny)], xrecv, dx, 0)
+
+    combine_face(ybuf.at[1], ycon.at[1])
+
+    combine_face(ybuf.at[0], ycon.at[0])
+    early = jnp.logical_and(iy == 1, jnp.logical_not(odd))
+
+    def send_back():
+        transfer(ybuf.at[0], yland.at[1], yrecv, 0, -1)
+
+    pl.when(early)(send_back)
 
     @pl.loop(0, ze // 2)
     def _(half):
@@ -322,6 +379,12 @@
         v, total = around(rhs, z)
         it[z] = alpha * v + beta * total
 
+    @pl.when(odd)
+    def _():
+        transfer(ybuf.at[1], yland.at[0], yrecv, 0, 1)
+
+    pl.when(jnp.logical_not(early))(send_back)
+
     den_load.wait()
 
     @planes(h, nz + h, UNROLL)
@@ -332,12 +395,6 @@
             span = slice(t * SUB, (t + 1) * SUB)
             base[z - h, span, :] = blend(lambda i: dens[i, z - h, span, :]) + u[span, :]
 
-    _, c1, c2, c3 = neighbour_polynomial()
-
-    def by_distance(first, second, square):
-        near_by = (c1 + 3.0 * c3) * first + (2.0 * c2) * second + (3.0 * c3) * square
-        return near_by, c2 * first + (3.0 * c3) * second
-
     wide = ny + 2 * SUB
     inside = slice(SUB, SUB + ny)
     column = lax.broadcasted_iota(jnp.int32, (ny, nx), 1)
@@ -347,7 +404,7 @@
         total = pltpu.roll(d, h, 1) + pltpu.roll(d, nx - h, 1)
         return total + (pltpu.roll(d, 1, 0) + pltpu.roll(d, wide - 1, 0))
 
-    all_of(cland, csend, crecv).wait()
+    all_of(2 * ny + 4 * count, xrecv).wait_recv()
     sub = lax.broadcasted_iota(jnp.int32, (SUB, nx), 0)
     for s in range(2):
         for end, (start, nearest) in enumerate(((0, SUB - 1), (ny + SUB, 0))):
@@ -355,7 +412,6 @@
             land[s, start:start + SUB, :] = jnp.where(
                 sub == nearest, found, pltpu.roll(found, turn[s], 1)
             )
-    all_of(land.at[:, pl.ds(SUB, ny)], xsend, xrecv).wait()
 
     sides = []
     for s in range(2):
@@ -386,35 +442,21 @@
             v = pltpu.roll(xc[e % 2, span, :], (-(h * e + h)) % nx, 1)
             base[z, span, :] = base[z, span, :] + jnp.where(edge, v, 0.0)
 
-    all_of(yland.at[:, message], ysend, yrecv).wait()
-
-    along = lax.broadcasted_iota(jnp.int32, (zp, nx), 1)
-    at_first, at_last = along == 0, along == nx - 1
-
-    def face_sum(d):
-        total = jnp.where(at_first, 0.0, pltpu.roll(d, 1, 1))
-        total = total + jnp.where(at_last, 0.0, pltpu.roll(d, nx - 1, 1))
-        return total + (pltpu.roll(d, 1, 0) + pltpu.roll(d, zp - 1, 0))
-
-    for s in range(2):
-        d1, d2 = (
-            yland[s, k * zp:(k + 1) * zp, :] - ybuf[1 - s, k * zp:(k + 1) * zp, :]
-            for k in range(2)
-        )
-        d3 = yland[s, 2 * zp:2 * zp + nz, :] - ybuf[1 - s, 2 * zp:2 * zp + nz, :]
-        m = face_sum(d1)
-        mm = face_sum(m) + jnp.where(at_first | at_last, d1, 0.0)
-        near_1, near_2 = by_distance(d1[:nz], m[:nz], mm[:nz])
-        rows = [
-            near_1 + (c2 * d2 + (3.0 * c3) * face_sum(d2))[:nz] + c3 * d3,
-            near_2 + c3 * d2[:nz],
-            c3 * d1[:nz],
-        ]
-        for j, r in enumerate(rows):
-            p = j if s == 0 else 2 * SUB - 1 - j
-            yc[p * zp:p * zp + nz, :] = r
-
-    gram_all.wait_send()
+    all_of(2 * message_rows, yrecv).wait_recv()
+    for q in range(h):
+        rows = slice(q * nz, (q + 1) * nz)
+        for s, p in enumerate((q, 2 * SUB - h + q)):
+            yc[p * zp:p * zp + nz, :] = yland[s, rows, :] - ybuf[1 - s, rows, :]
+
+    rows = total_devices - 1 + 2 * count * h * ny + 4 * count + 2 * ny + message_rows
+
+    @pl.when(odd)
+    def _():
+        all_of(rows + 2 * message_rows, sent).wait_send()
+
+    @pl.when(jnp.logical_not(odd))
+    def _():
+        all_of(rows + mate_rows, sent).wait_send()
 
 
 def finish(base, yc, weights, out, wout, stage, sem, wsem):
@@ -450,9 +492,9 @@
     ze = nz + 2 * h
     zp = pl.cdiv(ze, SUB) * SUB
     n = counts[0] * counts[1] * counts[2]
-    chunks = 8
+    chunks = [nz // 8] * 8
     tiles = ny // SUB
-    assert tiles >= 2 and h * (ze + 1) <= nx
+    assert tiles >= 2 and h * (ze + 1) <= nx and nz % 8 == 0 and counts[2] % 2 == 0
     dma = pltpu.SemaphoreType.DMA
     f32 = jnp.float32
     field = pltpu.VMEM((ze, ny, nx), f32)
@@ -479,10 +521,13 @@
             pltpu.VMEM((2, 2, count, nx), f32),
             pltpu.VMEM((2, 2, count, nx), f32),
             pltpu.VMEM((count, 2 * SUB * zp, nx), f32),
-            pltpu.VMEM((2, h * zp, nx), f32),
-            pltpu.VMEM((2, h * zp, nx), f32),
+            pltpu.VMEM((2, count, h * nz, nx), f32),
+            pltpu.VMEM((count, h * nz, nx), f32),
+            pltpu.VMEM((h * nz, nx), f32),
+            pltpu.VMEM((2, h * nz, nx), f32),
+            pltpu.VMEM((2, h * nz, nx), f32),
             pltpu.VMEM((2, ny, nx), f32),
-            dma((chunks,)), *(dma(()) for _ in range(11)),
+            dma((len(chunks),)), *(dma(()) for _ in range(7)),
         ],
         compiler_params=pltpu.CompilerParams(
             collective_id=0, has_side_effects=True, vmem_limit_bytes=56 * 1024 * 1024

time: 17.4 us -> 16.7 us (0.960)
  the two profiles are of different devices: /device:TPU:0 before, /device:TPU:1 now
where the time goes in v5:
time: 16.7 us; the launch traced here: 16.5 us
  Pallas kernels  15.9 us (95%)
  between operations  0.64 us (4%)
    pallas_call x1, Pallas kernels, on_device(): pl.pallas_call(functools.partial(kernel, counts, dims, chunks), out_shape...  15.1 us
    pallas_call x1, Pallas kernels, on_device(): pl.pallas_call(finish, out_shape=(jax.ShapeDtypeStruct((nz, ny, nx), f32)...  0.8 us

profile of v5, /device:TPU:1, one launch (start us, length us, event | category | flops | bytes accessed | tf_op | source)
XLA Modules:
  0.0 16.5 jit_solution(11710156147965403586)
XLA Ops:
  0.6 15.1 %shard_map.41 = (f32[32,32,128]{2,1,0:T(8,128)S(1)}, f32[640,128]{1,0:T(8,128)S(1)}, f32[1,7]{1,0:T(1,128)S(1)}) custom-call(f32[7,32,32,128]{3,2,1,0:T(8,128)} %res.1, f32[7,32,32,128]{3,2,1,0:T(8,128)} %den.1), custom_call_target="tpu_custom_call" | custom-call | tf_op jit(solution)/shard_map/pallas_call | solution.py:504
  15.7 0.8 %shard_map.42 = (f32[32,32,128]{2,1,0:T(8,128)}, f32[1,7]{1,0:T(1,128)}) custom-call(f32[32,32,128]{2,1,0:T(8,128)S(1)} %get-tuple-element.7.base, f32[640,128]{1,0:T(8,128)S(1)} %get-tuple-element.8.yc, f32[1,7]{1,0:T(1,128)S(1)} %get-tuple-element.9.weights), custom_call_target="tpu_custom_call" | custom-call | tf_op jit(solution)/shard_map/pallas_call | solution.py:536

commit v6 on v5

--- a/solution.py
+++ b/solution.py
@@ -86,7 +86,7 @@
         (dx, dy, dz) for dx in range(cx) for dy in range(cy) for dz in range(cz) if dx or dy or dz
     ]
     order = [1, cy - 1, *range(2, cy - 1), 0]
-    offsets.sort(key=lambda o: (-(o[0] % 2), order.index(o[1])))
+    offsets.sort(key=lambda o: (order.index(o[1]), -(o[0] % 2)))
     gx = [lax.rem(ix + d, cx) for d in range(cx)]
     gy = [lax.rem(iy + d, cy) for d in range(cy)]
     gz = [lax.rem(iz + d, cz) for d in range(cz)]
@@ -275,7 +275,10 @@
 
     all_of(total_devices - 1, grecv).wait_recv()
 
-    total = jnp.sum(slots[...], axis=0)
+    parts = [slots[k] for k in range(total_devices)]
+    while len(parts) > 1:
+        parts = [sum(parts[k + 1:k + 2], parts[k]) for k in range(0, len(parts), 2)]
+    total = parts[0]
 
     g = {}
     for p, (i, j) in enumerate(pairs):
@@ -297,7 +300,8 @@
     norm = solved[0]
     for k in range(1, count):
         norm = norm + solved[k]
-    weights = [s / norm for s in solved]
+    scale = 1.0 / norm
+    weights = [s * scale for s in solved]
 
     def blend(parts):
         s = weights[0] * parts(0)
@@ -374,14 +378,17 @@
         v, total = around(comb, z)
         rhs[z] = 6.0 * v - total
 
-    @planes(2, ze - 2, UNROLL)
-    def _(z):
+    def second_pass(z):
         v, total = around(rhs, z)
         it[z] = alpha * v + beta * total
+
+    planes(2, 2 + 12, UNROLL)(second_pass)
 
     @pl.when(odd)
     def _():
         transfer(ybuf.at[1], yland.at[0], yrecv, 0, 1)
+
+    planes(2 + 12, ze - 2, UNROLL)(second_pass)
 
     pl.when(jnp.logical_not(early))(send_back)
 

time: 16.7 us -> 16.4 us (0.982)
  the two profiles are of different devices: /device:TPU:1 before, /device:TPU:0 now
where the time goes in v6:
time: 16.4 us; the launch traced here: 16.2 us
  Pallas kernels  15.5 us (95%)
  between operations  0.64 us (4%)
    pallas_call x1, Pallas kernels, on_device(): pl.pallas_call(functools.partial(kernel, counts, dims, chunks), out_shape...  14.7 us
    pallas_call x1, Pallas kernels, on_device(): pl.pallas_call(finish, out_shape=(jax.ShapeDtypeStruct((nz, ny, nx), f32)...  0.8 us

profile of v6, /device:TPU:0, one launch (start us, length us, event | category | flops | bytes accessed | tf_op | source)
XLA Modules:
  0.0 16.2 jit_solution(15229758287971917060)
XLA Ops:
  0.6 14.7 %shard_map.41 = (f32[32,32,128]{2,1,0:T(8,128)S(1)}, f32[640,128]{1,0:T(8,128)S(1)}, f32[1,7]{1,0:T(1,128)S(1)}) custom-call(f32[7,32,32,128]{3,2,1,0:T(8,128)} %res.1, f32[7,32,32,128]{3,2,1,0:T(8,128)} %den.1), custom_call_target="tpu_custom_call" | custom-call | tf_op jit(solution)/shard_map/pallas_call | solution.py:511
  15.4 0.8 %shard_map.42 = (f32[32,32,128]{2,1,0:T(8,128)}, f32[1,7]{1,0:T(1,128)}) custom-call(f32[32,32,128]{2,1,0:T(8,128)S(1)} %get-tuple-element.7.base, f32[640,128]{1,0:T(8,128)S(1)} %get-tuple-element.8.yc, f32[1,7]{1,0:T(1,128)S(1)} %get-tuple-element.9.weights), custom_call_target="tpu_custom_call" | custom-call | tf_op jit(solution)/shard_map/pallas_call | solution.py:543

commit v7 on v6

--- a/solution.py
+++ b/solution.py
@@ -130,7 +130,7 @@
             device_id_type=MESH,
         )
 
-    for dx, dy, dz in sorted(offsets, key=lambda o: (-(o[0] % 2), order.index(-o[1] % cy))):
+    for dx, dy, dz in sorted(offsets, key=lambda o: -sum(min(d, c - d) for d, c in zip(o, counts))):
         gram_copy(dx, dy, dz).start()
 
     flat_held = held.reshape(count * ze * ny, nx)
@@ -146,17 +146,6 @@
             device_id_type=MESH,
         )
 
-    for k, (start, dest, dz) in enumerate(((h, nz + h, -1), (nz, 0, 1))):
-        cp = pltpu.make_async_remote_copy(
-            src_ref=held.at[:, pl.ds(start, h)],
-            dst_ref=held.at[:, pl.ds(dest, h)],
-            send_sem=sent,
-            recv_sem=zrecv,
-            device_id=near(0, 0, dz),
-            device_id_type=MESH,
-        )
-        cp.start()
-
     def transfer(source, target, recv_sem, dx, dy, dz=0):
         pltpu.make_async_remote_copy(
             src_ref=source,
@@ -187,12 +176,26 @@
 
     inner, outer = range(h, nz + h), (*range(h), *range(nz + h, ze))
 
-    @pl.loop(0, count)
-    def _(i):
+    def gather_inner(i):
         gather_y(i, 1, inner)
         zero = jnp.zeros((SUB, nx), jnp.float32)
         for t in range(tiles):
             gather_x(i, t, inner, zero, zero)
+
+    pl.loop(0, 1)(gather_inner)
+
+    for k, (start, dest, dz) in enumerate(((h, nz + h, -1), (nz, 0, 1))):
+        cp = pltpu.make_async_remote_copy(
+            src_ref=held.at[:, pl.ds(start, h)],
+            dst_ref=held.at[:, pl.ds(dest, h)],
+            send_sem=sent,
+            recv_sem=zrecv,
+            device_id=near(0, 0, dz),
+            device_id_type=MESH,
+        )
+        cp.start()
+
+    pl.loop(1, count)(gather_inner)
 
     all_of(2 * count * h * ny, zrecv).wait_recv()
     for i in range(count):

time: 16.4 us -> 16.5 us (level)
  the two profiles are of different devices: /device:TPU:0 before, /device:TPU:1 now
where the time goes in v7:
time: 16.5 us; the launch traced here: 16.3 us
  Pallas kernels  15.7 us (95%)
  between operations  0.64 us (4%)
    pallas_call x1, Pallas kernels, on_device(): pl.pallas_call(functools.partial(kernel, counts, dims, chunks), out_shape...  14.9 us
    pallas_call x1, Pallas kernels, on_device(): pl.pallas_call(finish, out_shape=(jax.ShapeDtypeStruct((nz, ny, nx), f32)...  0.8 us

profile of v7, /device:TPU:1, one launch (start us, length us, event | category | flops | bytes accessed | tf_op | source)
XLA Modules:
  0.0 16.3 jit_solution(509030772224810388)
XLA Ops:
  0.6 14.9 %shard_map.41 = (f32[32,32,128]{2,1,0:T(8,128)S(1)}, f32[640,128]{1,0:T(8,128)S(1)}, f32[1,7]{1,0:T(1,128)S(1)}) custom-call(f32[7,32,32,128]{3,2,1,0:T(8,128)} %res.1, f32[7,32,32,128]{3,2,1,0:T(8,128)} %den.1), custom_call_target="tpu_custom_call" | custom-call | tf_op jit(solution)/shard_map/pallas_call | solution.py:514
  15.5 0.8 %shard_map.42 = (f32[32,32,128]{2,1,0:T(8,128)}, f32[1,7]{1,0:T(1,128)}) custom-call(f32[32,32,128]{2,1,0:T(8,128)S(1)} %get-tuple-element.7.base, f32[640,128]{1,0:T(8,128)S(1)} %get-tuple-element.8.yc, f32[1,7]{1,0:T(1,128)S(1)} %get-tuple-element.9.weights), custom_call_target="tpu_custom_call" | custom-call | tf_op jit(solution)/shard_map/pallas_call | solution.py:546
